TPU v7x, 256 devices: a whole 4x4x8 slice. The times are simulated.
256 devices in a mesh: side: 2 (over y_hi), grp: 64 (over z, y_lo, x), rep: 2 (over core).
Axes of the slice: x: 4, y: 4 (y_hi: 2, y_lo: 2; y = y_hi * 2 + y_lo), z: 8, core: 2. Of those that a mesh axis runs over, the one named last changes fastest.
Arguments:
- hidden_in: bfloat16 [64, 12288], replicated, may hold values from -6 to 6
- norm_gain: float32 [12288], replicated, may hold values from 0.2 to 1.8
- qkv_weight: bfloat16 [12288, 14336], P('side', ('grp', 'rep')), may hold values from -0.0546875 to 0.0546875
- out_weight: bfloat16 [12288, 12288], P(('grp', 'rep'), 'side'), may hold values from -0.21875 to 0.21875
- gate_weight: bfloat16 [12288, 17408], P('side', ('grp', 'rep')), may hold values from -0.0546875 to 0.0546875
- up_weight: bfloat16 [12288, 17408], P('side', ('grp', 'rep')), may hold values from -0.0546875 to 0.0546875
- down_weight: bfloat16 [17408, 12288], P(('grp', 'rep'), 'side'), may hold values from -0.1875 to 0.1875
- cache_keys: bfloat16 [512, 4096, 128], P(('side', 'grp', 'rep')), may hold values from -1500 to 1500, as said below
- cache_values: bfloat16 [512, 4096, 128], P(('side', 'grp', 'rep')), may hold values from -6 to 6
- positions: int32 [64], replicated, may hold values from 0 to 4095
- write_slots: int32 [64], replicated, may hold values from 0 to 4095
Outputs:
- mixed: bfloat16 [64, 12288], P(None, ('side', 'grp', 'rep'))
Inputs may be any that keep to these rules, and one draw needn't show every extreme that they name: `cache_keys`: stored keys, already rotated at their own positions. `positions`: the row's cache holds position + 1 used slots, ending at its write slot.
All inputs are finite; a program needn't handle non-finite values.
Results may differ from a plain program's by a relative error of at most 0.012.
Values may be sent and summed in bfloat16 or wider, within the bound.
A program may use at most 64 MiB of HBM per device.

v0:
```python
import math

import jax
import jax.numpy as jnp
from jax import lax
from jax.sharding import Mesh
from jax.sharding import PartitionSpec as P

KVH = 8
HD = 128
SIDE_GRP_REP = ("side", "grp_0", "grp_1", "grp_2", "rep")
GRP = ("grp_0", "grp_1", "grp_2")
GRP_REP = ("grp_0", "grp_1", "grp_2", "rep")


EPSILON = 1e-05
THETA = 50000.0
MASKED = -1e30


def from_partner(value, axis, apart):
    mask = 2**apart
    pairs = [(source, source ^ mask) for source in range(lax.axis_size(axis))]
    return lax.ppermute(value, axis, pairs)


def in_blocks(array, dim, size):
    dims = array.shape
    tiles = array.reshape(*dims[:dim], size, dims[dim] // size, *dims[dim + 1 :])
    return jnp.moveaxis(tiles, dim, 0)


def sent_and_summed(array, axis, dim):
    tiles = in_blocks(array, dim, lax.axis_size(axis))
    arrived = lax.all_to_all(tiles, axis, split_axis=0, concat_axis=0, tiled=True)
    return arrived.sum(axis=0)


def copy_for_each(array, axis):
    size = lax.axis_size(axis)
    return lax.all_to_all(
        jnp.broadcast_to(array[None], (size, *array.shape)), axis, 0, 0, tiled=True
    )


def joined_along(tiles, dim):
    dims = list(tiles.shape[1:])
    dims[dim] *= tiles.shape[0]
    return jnp.moveaxis(tiles, 0, dim).reshape(dims)


def whole_of(array, axes, dim):
    far, near = axes
    leading = copy_for_each(array, far)
    tiles = jnp.swapaxes(copy_for_each(leading, near), 0, 1)
    return joined_along(tiles.reshape(-1, *array.shape), dim)


def of_everyone(array, axis):
    everything = copy_for_each(array, axis)
    return jnp.sum(everything, axis=0)


def in_one(arrays, axis):
    ends = [0]
    for a in arrays:
        ends.append(ends[-1] + a.size)
    so_far = of_everyone(jnp.concatenate([a.ravel() for a in arrays]), axis)
    return tuple((so_far[b:e].reshape(a.shape) for a, b, e in zip(arrays, ends, ends[1:])))


def sum_in_two_steps(array, axes, dim):
    far, near = axes
    own = sent_and_summed(in_blocks(array, dim, lax.axis_size(far)), near, dim + 1)
    return jnp.sum(lax.all_to_all(own, far, 0, 0, tiled=True), axis=0)


def normalize(rows_in, norm_gain):
    values = rows_in.astype(jnp.float32)
    center = jnp.mean(values, axis=-1, keepdims=True)
    spread = jnp.mean(jnp.square(values - center), axis=-1, keepdims=True)
    return ((values - center) * lax.rsqrt(spread + EPSILON) * norm_gain).astype(jnp.bfloat16)


def rotate(values, positions):
    half_width = values.shape[-1] // 2
    frequency = THETA ** (-2.0 * jnp.arange(half_width, dtype=jnp.float32) / values.shape[-1])
    angles = positions.astype(jnp.float32)[:, None] * frequency[None, :]
    cosine = jnp.cos(angles)[:, None, :]
    sine_part = jnp.sin(angles)[:, None, :]
    first_half = values[..., :half_width]
    second_half = values[..., half_width:]
    return jnp.concatenate(
        [
            first_half * cosine - second_half * sine_part,
            second_half * cosine + first_half * sine_part,
        ],
        axis=-1,
    )


def attend(queries, cache_keys, cache_values, new_keys, new_values, row_positions, row_slots):
    window = cache_keys.shape[1]
    column = jnp.arange(window, dtype=jnp.int32)
    hit_slot = (column[None, :] == row_slots[:, None])[:, :, None]
    keys_now = jnp.where(hit_slot, new_keys[:, None, :], cache_keys)
    values_now = jnp.where(hit_slot, new_values[:, None, :], cache_values)
    scores = jnp.einsum("tpd,tjd->tpj", queries, keys_now, preferred_element_type=jnp.float32) * (
        1.0 / math.sqrt(queries.shape[-1])
    )
    usable = ((row_slots[:, None] - column[None, :]) % window <= row_positions[:, None])[:, None, :]
    scores = jnp.where(usable, scores, MASKED)
    highest = jnp.max(scores, axis=-1, keepdims=True)
    weights = jnp.exp(scores - highest)
    probs = (weights / jnp.sum(weights, axis=-1, keepdims=True)).astype(jnp.bfloat16)
    return jnp.einsum("tpj,tjd->tpd", probs, values_now, preferred_element_type=jnp.float32).astype(
        jnp.bfloat16
    )


def swap_heads(pieces, bit_index):
    return from_partner(pieces, SIDE_GRP_REP, bit_index)


def butterfly(pieces, device, bit_index, swapper):
    count = pieces.shape[0]
    span_size = 1 << bit_index
    shaped = pieces.reshape((count // (2 * span_size), 2, span_size) + pieces.shape[1:])
    own_bit = device >> bit_index & 1
    keep_half = lax.dynamic_index_in_dim(shaped, own_bit, 1, keepdims=True)
    send_half = lax.dynamic_index_in_dim(shaped, 1 - own_bit, 1, keepdims=True)
    received = swapper(send_half, bit_index)
    joined = jnp.where(
        own_bit == 0,
        jnp.concatenate([keep_half, received], 1),
        jnp.concatenate([received, keep_half], 1),
    )
    return joined.reshape(pieces.shape)


def body(
    hidden_in,
    norm_gain,
    qkv_weight,
    out_weight,
    gate_weight,
    up_weight,
    down_weight,
    cache_keys,
    cache_values,
    positions,
    write_slots,
):
    side_count = lax.axis_size("side")
    group_count = lax.axis_size(GRP)
    replica_count = lax.axis_size("rep")
    device_count = side_count * group_count * replica_count
    device = lax.axis_index(SIDE_GRP_REP)
    side_index = lax.axis_index("side")
    inner_index = lax.axis_index(GRP_REP)
    normed = normalize(hidden_in, norm_gain)
    row_groups = group_count // KVH
    local_span = row_groups * replica_count
    per_device = cache_keys.shape[0]
    half_width = qkv_weight.shape[0]
    normed_half = lax.dynamic_slice_in_dim(normed, side_index * half_width, half_width, 1)
    term = jnp.dot(normed_half, qkv_weight, preferred_element_type=jnp.float32)
    batch_columns = sent_and_summed(term, "side", 0).astype(jnp.bfloat16)
    every_column = whole_of(batch_columns, (("grp_0", "grp_1", "grp_2"), "rep"), 1)
    own_rows = lax.dynamic_slice_in_dim(
        every_column, inner_index % local_span * per_device, per_device, 0
    )
    shaped_rows = own_rows.reshape(per_device, -1, KVH, HD)
    own_columns = lax.dynamic_index_in_dim(
        shaped_rows, inner_index // local_span, 2, keepdims=False
    )
    projected = lax.optimization_barrier(own_columns)
    head_count = projected.shape[1] - 2
    row_start = side_index * (local_span * per_device) + inner_index % local_span * per_device
    row_positions = lax.dynamic_slice_in_dim(positions, row_start, per_device)
    row_slots = lax.dynamic_slice_in_dim(write_slots, row_start, per_device)
    queries = rotate(projected[:, :head_count].astype(jnp.float32), row_positions).astype(
        jnp.bfloat16
    )
    new_keys = rotate(
        projected[:, head_count : head_count + 1].astype(jnp.float32), row_positions
    ).astype(jnp.bfloat16)[:, 0]
    new_values = projected[:, head_count + 1]
    attended = attend(
        queries, cache_keys, cache_values, new_keys, new_values, row_positions, row_slots
    )
    block_width = out_weight.shape[0]
    pieces = jnp.swapaxes(attended.reshape(per_device, local_span, block_width), 0, 1)
    for bit_index in range(local_span.bit_length() - 1):
        pieces = butterfly(pieces, device, bit_index, swap_heads)
    head_block = pieces.reshape(-1, block_width)
    bit_index = 7
    partner = swap_heads(head_block, bit_index)
    own_bit = device >> bit_index & 1
    head_block = jnp.where(
        own_bit == 0,
        jnp.concatenate([head_block, partner], 0),
        jnp.concatenate([partner, head_block], 0),
    )
    from_heads = jnp.dot(head_block, out_weight, preferred_element_type=jnp.float32)
    gate_sum = jnp.dot(normed_half, gate_weight, preferred_element_type=jnp.float32)
    up_sum = jnp.dot(normed_half, up_weight, preferred_element_type=jnp.float32)
    gate_sum, up_sum = in_one((gate_sum, up_sum), "side")
    activated = (jax.nn.silu(gate_sum) * up_sum).astype(jnp.bfloat16)
    from_units = jnp.dot(activated, down_weight, preferred_element_type=jnp.float32)
    summed = sum_in_two_steps(from_heads + from_units, (("grp_0", "grp_1", "grp_2"), "rep"), 1)
    out_width = summed.shape[1]
    residual = lax.dynamic_slice_in_dim(hidden_in, device * out_width, out_width, 1)
    return (residual.astype(jnp.float32) + summed).astype(jnp.bfloat16)


def solution(mesh):
    split = Mesh(
        mesh.devices.reshape(mesh.shape["side"], 8, 2, 4, mesh.shape["rep"]),
        ("side", "grp_0", "grp_1", "grp_2", "rep"),
    )
    placed = (
        P(),
        P(),
        P("side", GRP_REP),
        P(GRP_REP, "side"),
        P("side", GRP_REP),
        P("side", GRP_REP),
        P(GRP_REP, "side"),
        P(SIDE_GRP_REP, None, None),
        P(SIDE_GRP_REP, None, None),
        P(),
        P(),
    )
    return jax.shard_map(
        body, mesh=split, in_specs=placed, out_specs=P(None, SIDE_GRP_REP), check_vma=False
    )
```

profile of v0, /device:TPU:1, one launch (start us, length us, event | category | flops | bytes accessed | tf_op | source)
XLA Modules:
  0.0 154.7 jit_solution(6754471408544013671)
XLA Ops:
  0.0 1.9 %convert_reduce_fusion = f32[64]{0:T(128)S(1)} fusion(bf16[64,12288]{1,0:T(8,128)(2,1)} %param.11), kind=kLoop, calls=%fused_computation.7 | loop fusion | flops 1572800 | bytes 1573120 | tf_op jit(solution)/shard_map/reduce_sum | solution.py:80
  2.0 2.2 %multiply_reduce_fusion = (f32[64]{0:T(128)S(1)}, f32[64,12288]{1,0:T(8,128)}) fusion(f32[64]{0:T(128)S(1)} %broadcast_multiply_fusion, bf16[64,12288]{1,0:T(8,128)(2,1)S(1)} %copy-done.1), kind=kLoop, calls=%fused_computation.8 | loop fusion | flops 3145664 | bytes 4719104 | tf_op jit(solution)/shard_map/reduce_sum | solution.py:81
  4.3 1.6 %fusion.10 = bf16[64,6144]{1,0:T(8,128)(2,1)S(1)} fusion(f32[64,12288]{1,0:T(8,128)} %get-tuple-element.8, s32[]{:T(128)S(6)} %select_n.151, f32[6144]{0:T(1024)S(1)} %dynamic-slice, f32[64]{0:T(128)S(1)} %add_rsqrt_fusion), kind=kLoop, calls=%fused_computation.16 | loop fusion | flops 1179648 | bytes 2384132 | tf_op jit(solution)/shard_map/convert_element_type | solution.py:82
  5.9 2.6 %fusion.50 = f32[64,112]{1,0:T(8,128)} fusion(bf16[64,6144]{1,0:T(8,128)(2,1)S(1)} %fusion.10, bf16[6144,112]{0,1:T(8,128)(2,1)} %param.13), kind=kOutput, calls=%fused_computation.92 | convolution fusion | flops 88080384 | bytes 2191360 | tf_op jit(solution)/shard_map/dot_general | solution.py:167
  8.5 5.1 %all-to-all-start = ((f32[2,32,112]{2,1,0:T(8,128)}), f32[2,32,112]{2,1,0:T(8,128)S(1)}, u32[]{:S(2)}, u32[]{:S(2)}) async-start(f32[2,32,112]{2,1,0:T(8,128)} %bitcast), calls=%async_computation | async-start | bytes 65536 | tf_op jit(solution)/shard_map/all_to_all | solution.py:35
  13.6 2.8 %fusion.51 = f32[64,136]{1,0:T(8,128)} fusion(bf16[64,6144]{1,0:T(8,128)(2,1)S(1)} %fusion.10, bf16[6144,136]{0,1:T(8,128)(2,1)} %param.15), kind=kOutput, calls=%fused_computation.93 | convolution fusion | flops 106954752 | bytes 2492416 | tf_op jit(solution)/shard_map/dot_general | solution.py:206
  16.5 1.4 all-to-all-done
  18.8 11.8 %all-to-all-start.1 = ((bf16[64,32,112]{2,1,0:T(8,128)(2,1)}), bf16[64,32,112]{2,1,0:T(8,128)(2,1)S(1)}, u32[]{:S(2)}, u32[]{:S(2)}) async-start(bf16[64,32,112]{2,1,0:T(8,128)(2,1)} %broadcast_in_dim.41), calls=%async_computation.1 | async-start | bytes 1048576 | tf_op jit(solution)/shard_map/all_to_all | solution.py:41
  31.0 13.8 %all-to-all-done.1 = bf16[64,32,112]{2,1,0:T(8,128)(2,1)S(1)} async-done(((bf16[64,32,112]{2,1,0:T(8,128)(2,1)}), bf16[64,32,112]{2,1,0:T(8,128)(2,1)S(1)}, u32[]{:S(2)}, u32[]{:S(2)}) %all-to-all-start.1) | async-done | bytes 458784 | tf_op jit(solution)/shard_map/all_to_all | solution.py:41
  44.9 9.1 %all_to_all.31 = bf16[2,64,32,112]{3,2,1,0:T(8,128)(2,1)S(1)} all-to-all(bf16[2,64,32,112]{3,2,1,0:T(8,128)(2,1)S(1)} %broadcast_in_dim.46), channel_id=1, replica_groups=mesh['side'=2,'grp_0'=8,'grp_1'=2,'grp_2'=4,'rep'=2] {'rep'}, dimensions={0} | all-to-all | bytes 1835008 | tf_op jit(solution)/shard_map/all_to_all | solution.py:41
  54.6 3.2 %reshape.311 = bf16[32,14336]{1,0:T(8,128)(2,1)} reshape(bf16[32,128,112]{2,1,0:T(8,128)(2,1)S(1)} %copy.51) | data formatting | bytes 1835008 | tf_op jit(solution)/shard_map/reshape | solution.py:49
  59.2 3.1 %fusion.45 = (f32[2,12]{1,0:T(2,128)S(1)}, f32[2,12,4096]{2,1,0:T(8,128)S(1)}) fusion(bf16[2,4096,128]{2,1,0:T(8,128)(2,1)} %param.18, pred[2,4096]{1,0:T(4,128)(4,1)S(1)} %get-tuple-element.28, bf16[2,128]{1,0:T(2,128)(2,1)S(1)} %pad_maximum_fusion.1, pred[2,4096]{1,0:T(4,128)(4,1)S(1)} %get-tuple-element.27, ...), kind=kOutput, calls=%fused_computation.88 | convolution fusion | flops 26624000 | bytes 2513504 | tf_op jit(solution)/shard_map/sub | solution.py:114
  62.3 3.5 %fusion.11 = bf16[2,12,128]{2,1,0:T(8,128)(2,1)S(1)} fusion(bf16[2,4096,128]{2,1,0:T(8,128)(2,1)} %param.19, pred[2,4096]{1,0:T(4,128)(4,1)S(1)} %get-tuple-element.28, bf16[2,128]{1,0:T(2,128)(2,1)S(1)} %get-tuple-element.22, f32[2,12,4096]{2,1,0:T(8,128)S(1)} %get-tuple-element.30, f32[2,12]{1,0:T(2,128)S(1)} %get-tuple-element.29), kind=kOutput, calls=%fused_computation.17 | convolution fusion | flops 26414080 | bytes 2505312 | tf_op jit(solution)/shard_map/tpj,tjd->tpd/dot_general | solution.py:116
  66.4 2.1 %fusion.52 = f32[64,136]{1,0:T(8,128)S(1)} fusion(bf16[64,6144]{1,0:T(8,128)(2,1)S(1)} %fusion.10, bf16[6144,136]{0,1:T(8,128)(2,1)} %param.16), kind=kOutput, calls=%fused_computation.94 | convolution fusion | flops 106954752 | bytes 2492416 | tf_op jit(solution)/shard_map/dot_general | solution.py:207
  69.8 3.4 %all-to-all-start.3 = ((f32[2,1,17408]{2,1,0:T(1,128)}), f32[2,1,17408]{2,1,0:T(1,128)S(1)}, u32[]{:S(2)}, u32[]{:S(2)}) async-start(f32[2,1,17408]{2,1,0:T(1,128)} %broadcast_in_dim.84), calls=%async_computation.3 | async-start | bytes 278528 | tf_op jit(solution)/shard_map/all_to_all | solution.py:41
  73.4 2.7 %collective-permute-start.2 = (bf16[2,1,4,2,96]{4,3,2,1,0:T(2,128)(2,1)S(1)}, bf16[2,1,4,2,96]{4,3,2,1,0:T(2,128)(2,1)S(1)}, u32[]{:S(2)}, u32[]{:S(2)}) collective-permute-start(bf16[2,1,4,2,96]{4,3,2,1,0:T(2,128)(2,1)S(1)} %get-tuple-element.16), channel_id=1, source_target_pairs={{0,4},{1,5},{2,6},{3,7},{4,0},{5,1},{6,2},{7,3},{8,12},{9,13},{10,... | collective-permute-start | bytes 9224 | tf_op jit(solution)/shard_map/ppermute | solution.py:24
  76.1 2.0 %all-to-all-done.3 = f32[2,1,17408]{2,1,0:T(1,128)S(1)} async-done(((f32[2,1,17408]{2,1,0:T(1,128)}), f32[2,1,17408]{2,1,0:T(1,128)S(1)}, u32[]{:S(2)}, u32[]{:S(2)}) %all-to-all-start.3) | async-done | bytes 139296 | tf_op jit(solution)/shard_map/all_to_all | solution.py:41
  78.4 1.3 collective-permute-start.3
  81.0 2.3 %collective-permute-start.4 = (bf16[32,96]{1,0:T(8,128)(2,1)S(1)}, bf16[32,96]{1,0:T(8,128)(2,1)S(1)}, u32[]{:S(2)}, u32[]{:S(2)}) collective-permute-start(bf16[32,96]{1,0:T(8,128)(2,1)S(1)} %bitcast.58), channel_id=1, source_target_pairs={{0,128},{1,129},{2,130},{3,131},{4,132},{5,133},{6,134},{7,135},{8... | collective-permute-start | bytes 18440 | tf_op jit(solution)/shard_map/ppermute | solution.py:24
  83.8 1.4 collective-permute-done.4
  85.6 2.3 %copy.61 = f32[64,6144]{0,1:T(8,128)} copy(f32[64,6144]{1,0:T(8,128)S(1)} %convolution_add_fusion) | data formatting | bytes 3145728 | tf_op jit(solution)/shard_map/reshape | solution.py:29
  87.9 3.8 %copy.77 = f32[2,64,64,48]{2,3,1,0:T(8,128)} copy(f32[2,64,64,48]{2,3,0,1:T(8,128)} %bitcast.51) | data formatting | bytes 3145728 | tf_op jit(solution)/shard_map/transpose | solution.py:30
  91.6 4.3 %reshape.319 = f32[2,1,196608]{2,1,0:T(1,128)} reshape(f32[2,64,48,64]{3,2,1,0:T(8,128)} %bitcast.52) | data formatting | bytes 3145728
  95.9 9.9 %all_to_all.32 = f32[2,1,196608]{2,1,0:T(1,128)S(1)} all-to-all(f32[2,1,196608]{2,1,0:T(1,128)} %reshape.319), channel_id=1, replica_groups=mesh['side'=2,'grp_0'=8,'grp_1'=2,'grp_2'=4,'rep'=2] {'rep'}, dimensions={0} | all-to-all | bytes 3145728 | tf_op jit(solution)/shard_map/all_to_all | solution.py:35
  106.3 6.6 %reduce.1 = f32[2,196608]{1,0:T(2,128)} reduce(f32[2,1,196608]{2,1,0:T(1,128)S(1)} %all_to_all.32, f32[]{:T(128)} %broadcast.194), dimensions={1}, to_apply=%all_to_all.23.reduce_sub_computation | reduce | bytes 3145732 | tf_op jit(solution)/shard_map/all_to_all | solution.py:35
  112.9 4.8 %reshape.320 = f32[2,64,48,64]{3,2,1,0:T(8,128)} reshape(f32[2,196608]{1,0:T(2,128)} %reduce.1) | data formatting | bytes 3145728
  117.7 2.3 %bitcast_reduce_fusion = f32[64,64,48]{1,2,0:T(8,128)S(1)} fusion(f32[2,64,48,64]{3,2,1,0:T(8,128)} %reshape.320), kind=kLoop, calls=%fused_computation.89 | loop fusion | flops 196608 | bytes 2359296 | tf_op jit(solution)/shard_map/reduce_sum | solution.py:36
  120.1 1.9 %reshape.321 = f32[64,1,3072]{2,1,0:T(1,128)} reshape(f32[64,48,64]{2,1,0:T(8,128)S(1)} %bitcast.53) | data formatting | bytes 1572864
  121.9 5.9 %all-to-all-start.5 = ((f32[64,1,3072]{2,1,0:T(1,128)}), f32[64,1,3072]{2,1,0:T(1,128)S(1)}, u32[]{:S(2)}, u32[]{:S(2)}) async-start(f32[64,1,3072]{2,1,0:T(1,128)} %reshape.321), calls=%async_computation.5 | async-start | bytes 1572864 | tf_op jit(solution)/shard_map/all_to_all | solution.py:75
  128.7 20.1 %all-to-all-done.5 = f32[64,1,3072]{2,1,0:T(1,128)S(1)} async-done(((f32[64,1,3072]{2,1,0:T(1,128)}), f32[64,1,3072]{2,1,0:T(1,128)S(1)}, u32[]{:S(2)}, u32[]{:S(2)}) %all-to-all-start.5) | async-done | bytes 786464 | tf_op jit(solution)/shard_map/all_to_all | solution.py:75
  148.8 3.6 %reduce.2 = f32[64,3072]{1,0:T(8,128)} reduce(f32[64,1,3072]{2,1,0:T(1,128)S(1)} %all-to-all-done.5, f32[]{:T(128)} %broadcast.194), dimensions={1}, to_apply=%all_to_all.24.reduce_sub_computation | reduce | bytes 1572868 | tf_op jit(solution)/shard_map/all_to_all | solution.py:75
  152.4 1.5 reshape.322
  (70 shorter events, 9.9 us)
Async XLA Ops:
  0.0 83.3 %copy-start = (bf16[136,6144]{1,0:T(8,128)(2,1)S(1)}, bf16[136,6144]{1,0:T(8,128)(2,1)}, u32[]{:S(2)}) copy-start(bf16[136,6144]{1,0:T(8,128)(2,1)} %param.17) | copy-start | bytes 5013508
  0.0 2.0 %copy-start.1 = (bf16[64,12288]{1,0:T(8,128)(2,1)S(1)}, bf16[64,12288]{1,0:T(8,128)(2,1)}, u32[]{:S(2)}) copy-start(bf16[64,12288]{1,0:T(8,128)(2,1)} %param.11) | copy-start | bytes 4718596
  2.0 2.2 %copy-start.4 = (f32[12288]{0:T(1024)S(1)}, f32[12288]{0:T(1024)}, u32[]{:S(2)}) copy-start(f32[12288]{0:T(1024)} %param.12) | copy-start | bytes 147460
  8.5 7.9 %copy-start.5 = (s32[64]{0:T(128)S(1)}, s32[64]{0:T(128)}, u32[]{:S(2)}) copy-start(s32[64]{0:T(128)} %param.20) | copy-start | bytes 772
  8.5 9.4 %all-to-all-start = ((f32[2,32,112]{2,1,0:T(8,128)}), f32[2,32,112]{2,1,0:T(8,128)S(1)}, u32[]{:S(2)}, u32[]{:S(2)}) async-start(f32[2,32,112]{2,1,0:T(8,128)} %bitcast), calls=%async_computation | async-start | bytes 65536 | tf_op jit(solution)/shard_map/all_to_all | solution.py:35
  13.6 17.1 %copy-start.6 = (s32[64]{0:T(128)S(1)}, s32[64]{0:T(128)}, u32[]{:S(2)}) copy-start(s32[64]{0:T(128)} %param.21) | copy-start | bytes 772
  18.8 26.0 %all-to-all-start.1 = ((bf16[64,32,112]{2,1,0:T(8,128)(2,1)}), bf16[64,32,112]{2,1,0:T(8,128)(2,1)S(1)}, u32[]{:S(2)}, u32[]{:S(2)}) async-start(bf16[64,32,112]{2,1,0:T(8,128)(2,1)} %broadcast_in_dim.41), calls=%async_computation.1 | async-start | bytes 1048576 | tf_op jit(solution)/shard_map/all_to_all | solution.py:41
  65.8 2.7 %copy-start.3 = (f32[64,136]{1,0:T(8,128)S(1)}, f32[64,136]{1,0:T(8,128)}, u32[]{:S(2)}) copy-start(f32[64,136]{1,0:T(8,128)} %fusion.51) | copy-start | bytes 104452
  66.0 2.8 %collective-permute-start = (bf16[8,1,1,2,96]{4,0,3,2,1:T(8,128)(2,1)S(1)}, bf16[8,1,1,2,96]{4,0,3,2,1:T(8,128)(2,1)S(1)}, u32[]{:S(2)}, u32[]{:S(2)}) collective-permute-start(bf16[8,1,1,2,96]{4,0,3,2,1:T(8,128)(2,1)S(1)} %copy.67), channel_id=1, source_target_pairs={{0,1},{1,0},{2,3},{3,2},{4,5},{5,4},{6,7},{7,6},{8,9},{9,8},{10,11... | collective-permute-start | bytes 9224 | tf_op jit(solution)/shard_map/ppermute | solution.py:24
  68.9 4.4 %collective-permute-start.1 = (bf16[4,1,2,2,96]{4,1,0,3,2:T(2,128)(2,1)S(1)}, bf16[4,1,2,2,96]{4,1,0,3,2:T(2,128)(2,1)S(1)}, u32[]{:S(2)}, u32[]{:S(2)}) collective-permute-start(bf16[4,1,2,2,96]{4,1,0,3,2:T(2,128)(2,1)S(1)} %get-tuple-element.18), channel_id=1, source_target_pairs={{0,2},{1,3},{2,0},{3,1},{4,6},{5,7},{6,4},{7,5},{8,10},{9,11},{10,... | collective-permute-start | bytes 9224 | tf_op jit(solution)/shard_map/ppermute | solution.py:24
  69.8 8.3 %all-to-all-start.3 = ((f32[2,1,17408]{2,1,0:T(1,128)}), f32[2,1,17408]{2,1,0:T(1,128)S(1)}, u32[]{:S(2)}, u32[]{:S(2)}) async-start(f32[2,1,17408]{2,1,0:T(1,128)} %broadcast_in_dim.84), calls=%async_computation.3 | async-start | bytes 278528 | tf_op jit(solution)/shard_map/all_to_all | solution.py:41
  73.4 4.9 %collective-permute-start.2 = (bf16[2,1,4,2,96]{4,3,2,1,0:T(2,128)(2,1)S(1)}, bf16[2,1,4,2,96]{4,3,2,1,0:T(2,128)(2,1)S(1)}, u32[]{:S(2)}, u32[]{:S(2)}) collective-permute-start(bf16[2,1,4,2,96]{4,3,2,1,0:T(2,128)(2,1)S(1)} %get-tuple-element.16), channel_id=1, source_target_pairs={{0,4},{1,5},{2,6},{3,7},{4,0},{5,1},{6,2},{7,3},{8,12},{9,13},{10,... | collective-permute-start | bytes 9224 | tf_op jit(solution)/shard_map/ppermute | solution.py:24
  78.4 2.5 %collective-permute-start.3 = (bf16[1,1,8,2,96]{4,3,2,1,0:T(2,128)(2,1)S(1)}, bf16[1,1,8,2,96]{4,3,2,1,0:T(2,128)(2,1)S(1)}, u32[]{:S(2)}, u32[]{:S(2)}) collective-permute-start(bf16[1,1,8,2,96]{4,3,2,1,0:T(2,128)(2,1)S(1)} %get-tuple-element.14), channel_id=1, source_target_pairs={{0,8},{1,9},{2,10},{3,11},{4,12},{5,13},{6,14},{7,15},{8,0},{9,1},... | collective-permute-start | bytes 9224 | tf_op jit(solution)/shard_map/ppermute | solution.py:24
  80.9 4.3 %copy-start.2 = (bf16[96,6144]{1,0:T(8,128)(2,1)S(1)}, bf16[96,6144]{1,0:T(8,128)(2,1)}, u32[]{:S(2)}) copy-start(bf16[96,6144]{1,0:T(8,128)(2,1)} %param.14) | copy-start | bytes 3538948
  81.0 4.3 %collective-permute-start.4 = (bf16[32,96]{1,0:T(8,128)(2,1)S(1)}, bf16[32,96]{1,0:T(8,128)(2,1)S(1)}, u32[]{:S(2)}, u32[]{:S(2)}) collective-permute-start(bf16[32,96]{1,0:T(8,128)(2,1)S(1)} %bitcast.58), channel_id=1, source_target_pairs={{0,128},{1,129},{2,130},{3,131},{4,132},{5,133},{6,134},{7,135},{8... | collective-permute-start | bytes 18440 | tf_op jit(solution)/shard_map/ppermute | solution.py:24
  121.9 26.9 %all-to-all-start.5 = ((f32[64,1,3072]{2,1,0:T(1,128)}), f32[64,1,3072]{2,1,0:T(1,128)S(1)}, u32[]{:S(2)}, u32[]{:S(2)}) async-start(f32[64,1,3072]{2,1,0:T(1,128)} %reshape.321), calls=%async_computation.5 | async-start | bytes 1572864 | tf_op jit(solution)/shard_map/all_to_all | solution.py:75
where the time goes:
time: 157 us; the launch traced here: 155 us
  waiting for transfers between devices  39.7 us (25%)
  starting transfers between devices  33.2 us (21%)
  local copies, waits for them, and re-layouts  27.3 us (17%)
  other arithmetic  19.9 us (13%)
  blocking collectives  19 us (12%)
  matrix products  15 us (10%)
    all_to_all x1, waiting for transfers between devices, sum_in_two_steps(): return jnp.sum(lax.all_to_all(own, far, 0, 0, tiled=True), axis=0)  20.1 us
    all_to_all x2, waiting for transfers between devices, copy_for_each(): lax.all_to_all(jnp.broadcast_to(array[None], (size, *array.shape)), axis,...  15.8 us
    all_to_all x2, starting transfers between devices, copy_for_each(): lax.all_to_all(jnp.broadcast_to(array[None], (size, *array.shape)), axis,...  15.2 us
    unnamed x23, local copies, waits for them, and re-layouts  13.7 us
    all_to_all x1, blocking collectives, sent_and_summed(): lax.all_to_all(tiles, axis, split_axis=0, concat_axis=0, tiled=True)  9.92 us
    all_to_all x1, blocking collectives, copy_for_each(): lax.all_to_all(jnp.broadcast_to(array[None], (size, *array.shape)), axis,...  9.12 us
    ppermute x5, starting transfers between devices, from_partner(): return lax.ppermute(value, axis, pairs)  7.04 us
    all_to_all x1, other arithmetic, sent_and_summed(): lax.all_to_all(tiles, axis, split_axis=0, concat_axis=0, tiled=True)  6.61 us
  transfers between devices with their start and end apart: 9, of which 6 were waited for; matrix products, arithmetic and copies ran while one was open for 5% of the time, Pallas kernels for 0%

commit v1 on v0

v1 whole, which is shorter than its diff:
```python
import math

import jax
import jax.numpy as jnp
import numpy as np
from jax import lax
from jax.experimental import pallas as pl
from jax.experimental.pallas import tpu as pltpu
from jax.sharding import PartitionSpec as P

MESH = pl.DeviceIdType.MESH
D = 12288
HALF = 6144
EPSILON = 1e-05
THETA = 50000.0
MASKED = -1e30
WIN = 4096
HD = 128
COLS = 112
FFB = 136
OB = 96
NCOL = 3072
SCALE = 1.0 / math.sqrt(HD)
F32 = jnp.float32
BF16 = jnp.bfloat16
NT = (((1,), (1,)), ((), ()))
TN = (((0,), (0,)), ((), ()))


def kernel(
    hidden, gain, qkv, out_w, gate, up, down, keys, values, pos, slots, freq, out,
    hid_v, gain_v, qkv_v, wo_v, gate_v, up_v, wd_v, k_v, v_v, normed_v,
    send1, recv1, qrow, cs_v, att_v, recv2, lhs_v, gu_send, gu_recv, act_v, acc_v,
    p1send, recvp1, p2send, recvp2, res_v,
    load_sem, s1, r1, spre, rpre, s2, r2, s3, r3, s4, r4, sp1, rp1, sp2, rp2,
):
    s = lax.axis_index("side")
    g = lax.axis_index("grp")
    c = lax.axis_index("rep")
    z = g // 8
    chip = g % 8
    j = 2 * g + c
    d16 = 2 * chip + c
    row_off = 64 * (chip % 2)

    def load(src, dst, n):
        cp = pltpu.make_async_copy(src, dst, load_sem.at[n])
        cp.start()
        return cp

    hid_cp = load(hidden, hid_v, 0)
    gain_cp = load(gain, gain_v, 1)
    qkv_cp = load(qkv, qkv_v.at[pl.ds(0, COLS)], 2)
    gate_cp = load(gate, gate_v, 3)
    up_cp = load(up, up_v, 4)
    k_cp = load(keys, k_v, 5)
    v_cp = load(values, v_v, 6)
    own_cols = pl.ds(pl.multiple_of(NCOL * c, NCOL), NCOL)
    wo_cp = load(
        out_w.at[:, own_cols], wo_v.at[pl.ds(pl.multiple_of(row_off + OB * c, 32), OB)], 7
    )
    wd_cp = load(down.at[:, own_cols], wd_v.at[c], 8)

    barrier = pltpu.get_barrier_semaphore()

    def greet(n, carry):
        b, rest = n // 128, n % 128

        @pl.when(jnp.logical_not((b == s) & (rest == j)))
        def _():
            pl.semaphore_signal(
                barrier, inc=1, device_id=(b, rest // 2, rest % 2), device_id_type=MESH
            )

        return carry

    lax.fori_loop(0, 256, greet, 0)

    qkv_v[pl.ds(COLS, 16), :] = jnp.zeros((16, HALF), BF16)
    wo_v[pl.ds(pl.multiple_of(192 - 192 * (chip % 2), 64), 64), :] = jnp.zeros((64, NCOL), BF16)

    hid_cp.wait()

    def chunk(i):
        return hid_v[:, pl.ds(pl.multiple_of(i * 128, 128), 128)].astype(F32)

    total = lax.fori_loop(
        0, 96, lambda i, a: a + chunk(i), jnp.zeros((64, 128), F32), unroll=8
    )
    mean = jnp.sum(total, axis=1, keepdims=True) * (1.0 / D)

    def square(i, a):
        d = chunk(i) - mean
        return a + d * d

    spread = lax.fori_loop(0, 96, square, jnp.zeros((64, 128), F32), unroll=8)
    var = jnp.sum(spread, axis=1, keepdims=True) * (1.0 / D)
    rstd = lax.rsqrt(var + EPSILON)
    gain_cp.wait()

    def norm(i, carry):
        n = s * 48 + i
        v = (chunk(n) - mean) * rstd * gain_v[pl.ds(n, 1), :]
        normed_v[:, pl.ds(pl.multiple_of(i * 128, 128), 128)] = v.astype(BF16)
        return carry

    lax.fori_loop(0, 48, norm, 0, unroll=4)

    qkv_cp.wait()
    term = lax.dot_general(normed_v[...], qkv_v[...], NT, preferred_element_type=F32)
    m, t = j // 8, j % 8
    rolled = pltpu.roll(term, (128 - 16 * t) % 128, 1)
    lane = lax.broadcasted_iota(jnp.int32, (64, 128), 1)
    first = jnp.where(lane < COLS - 16 * t, rolled, 0.0)
    second = jnp.where(lane >= 128 - 16 * t, rolled, 0.0)
    for n in range(32):
        send1[n] = first[2 * n : 2 * n + 2]
        send1[32 + n] = second[2 * n : 2 * n + 2]

    pl.semaphore_wait(barrier, 255)

    valid = (t <= 6, t >= 1)
    for piece in range(2):
        q = jnp.maximum(7 * m + t - piece, 0)
        k, cc = q % 8, q // 8
        slot = jnp.minimum(cc, 13) * 4 + piece * 2 + s

        @pl.when(valid[piece])
        def _():
            def push(n, carry):
                b, i = n // 16, n % 16
                there = 8 * k + i // 2

                @pl.when(jnp.logical_not((b == s) & (there == g) & (i % 2 == c)))
                def _():
                    pltpu.make_async_remote_copy(
                        src_ref=send1.at[32 * piece + n],
                        dst_ref=recv1.at[slot],
                        send_sem=s1,
                        recv_sem=r1,
                        device_id=(b, there, i % 2),
                        device_id_type=MESH,
                    ).start()

                return carry

            lax.fori_loop(0, 32, push, 0)

            @pl.when(k == z)
            def _():
                recv1[slot] = send1[32 * piece + s * 16 + d16]

    other_cols = pl.ds(pl.multiple_of(NCOL * (1 - c), NCOL), NCOL)
    sibling = (s, g, 1 - c)
    pre_out = pltpu.make_async_remote_copy(
        src_ref=out_w.at[:, other_cols],
        dst_ref=wo_v.at[pl.ds(pl.multiple_of(row_off + OB * c, 32), OB)],
        send_sem=spre.at[0],
        recv_sem=rpre.at[0],
        device_id=sibling,
        device_id_type=MESH,
    )
    pre_out.start()
    pre_down = pltpu.make_async_remote_copy(
        src_ref=down.at[:, other_cols],
        dst_ref=wd_v.at[c],
        send_sem=spre.at[1],
        recv_sem=rpre.at[1],
        device_id=sibling,
        device_id_type=MESH,
    )
    pre_down.start()

    gate_cp.wait()
    gu_send[:, 0:64] = lax.dot_general(
        gate_v[...], normed_v[...], NT, preferred_element_type=F32
    )
    up_cp.wait()
    gu_send[:, 64:128] = lax.dot_general(
        up_v[...], normed_v[...], NT, preferred_element_type=F32
    )
    gu = pltpu.make_async_remote_copy(
        src_ref=gu_send,
        dst_ref=gu_recv,
        send_sem=s3,
        recv_sem=r3,
        device_id=(1 - s, g, c),
        device_id_type=MESH,
    )
    gu.start()

    col0 = 48 * (128 * s + j)
    tile = jnp.minimum(col0 // 128, 94)
    res_v[...] = hid_v[:, pl.ds(pl.multiple_of(tile * 128, 128), 256)].astype(F32).T
    res_off = pl.multiple_of(col0 - tile * 128, 16)

    lane1 = lax.broadcasted_iota(jnp.int32, (1, 128), 1)
    row0 = 32 * s + 2 * d16
    for r in range(2):
        angle = pos[row0 + r].astype(F32) * freq[...]
        sine = jnp.sin(angle)
        cs_v[2 * r : 2 * r + 1, :] = jnp.cos(angle)
        cs_v[2 * r + 1 : 2 * r + 2, :] = jnp.where(lane1 < 64, -sine, sine)
    qrow[...] = jnp.zeros((2, 16, 128), F32)

    mine = ((t <= 6) & ((7 * m + t) % 8 == z)) | ((t >= 1) & ((7 * m + t + 7) % 8 == z))

    def wait_recv(src, dst, send, recv):
        pltpu.make_async_remote_copy(
            src_ref=src, dst_ref=dst, send_sem=send, recv_sem=recv,
            device_id=sibling, device_id_type=MESH,
        ).wait_recv()

    def wait_send(src, dst, send, recv):
        pltpu.make_async_remote_copy(
            src_ref=src, dst_ref=dst, send_sem=send, recv_sem=recv,
            device_id=sibling, device_id_type=MESH,
        ).wait_send()

    @pl.when(mine)
    def _():
        part = recv1.at[pl.ds(0, 55)]
        wait_recv(part, part, s1, r1)

    @pl.when(jnp.logical_not(mine))
    def _():
        wait_recv(recv1, recv1, s1, r1)

    for cc in range(14):
        both = (recv1[4 * cc] + recv1[4 * cc + 1]) + (recv1[4 * cc + 2] + recv1[4 * cc + 3])
        both = both.astype(BF16).astype(F32)
        qrow[0, cc : cc + 1, :] = both[0:1]
        qrow[1, cc : cc + 1, :] = both[1:2]

    k_cp.wait()
    v_cp.wait()
    column = lax.broadcasted_iota(jnp.int32, (16, WIN), 1)
    for r in range(2):
        x = qrow[r]
        turned = x * cs_v[2 * r : 2 * r + 1, :] + pltpu.roll(x, 64, 1) * cs_v[2 * r + 1 : 2 * r + 2, :]
        query = turned.astype(BF16)
        rounded = query.astype(F32)
        new_key = rounded[12:13]
        new_value = x[13:14]
        slot_r = slots[row0 + r]
        pos_r = pos[row0 + r]
        hit = column == slot_r
        fresh = jnp.sum(rounded * new_key, axis=1, keepdims=True) * SCALE
        scores = lax.dot_general(query, k_v[r], NT, preferred_element_type=F32) * SCALE
        scores = jnp.where(hit, fresh, scores)
        usable = ((slot_r - column) & (WIN - 1)) <= pos_r
        scores = jnp.where(usable, scores, MASKED)
        highest = jnp.max(scores, axis=1, keepdims=True)
        weights = jnp.exp(scores - highest)
        denom = jnp.sum(weights, axis=1, keepdims=True)
        stale = jnp.where(hit, 0.0, weights).astype(BF16)
        summed = jnp.dot(stale, v_v[r], preferred_element_type=F32)
        own = jnp.exp(fresh - highest).astype(BF16).astype(F32)
        attended = ((summed + own * new_value) / denom).astype(BF16).astype(F32)
        for h in range(12):
            att_v[h, r : r + 1, :] = attended[h : h + 1]

    here = s * 16 + d16

    def spread_heads(n, carry):
        b, i = n // 16, n % 16
        u = i // 2

        @pl.when(jnp.logical_not((b == s) & (i == d16)))
        def _():
            pltpu.make_async_remote_copy(
                src_ref=att_v.at[pl.ds(3 * u // 2, 2)],
                dst_ref=recv2.at[here],
                send_sem=s2,
                recv_sem=r2,
                device_id=(b, 8 * z + u, i % 2),
                device_id_type=MESH,
            ).start()

        return carry

    lax.fori_loop(0, 32, spread_heads, 0)
    recv2[here] = att_v[pl.ds(3 * chip // 2, 2)]

    gu.wait()
    both = gu_send[...] + gu_recv[...]
    lane136 = lax.broadcasted_iota(jnp.int32, (FFB, 128), 1)
    active = both / (1.0 + jnp.exp(-both)) * pltpu.roll(both, 64, 1)
    act_v[c] = jnp.where(lane136 < 64, active, 0.0).astype(BF16)
    act_cp = pltpu.make_async_remote_copy(
        src_ref=act_v.at[c],
        dst_ref=act_v.at[c],
        send_sem=s4,
        recv_sem=r4,
        device_id=sibling,
        device_id_type=MESH,
    )
    act_cp.start()
    wd_cp.wait()
    pre_down.wait()
    act_cp.wait()
    for n in range(6):
        cols = slice(512 * n, 512 * n + 512)
        acc_v[:, cols] = lax.dot_general(
            act_v[0, :, 0:64], wd_v[0, :, cols], TN, preferred_element_type=F32
        ) + lax.dot_general(
            act_v[1, :, 0:64], wd_v[1, :, cols], TN, preferred_element_type=F32
        )
    wo_cp.wait()
    pre_out.wait()

    most = recv2.at[pl.ds(0, 31)]
    wait_recv(most, most, s2, r2)
    for n in range(32):
        lhs_v[2 * n : 2 * n + 2, 0:128] = recv2[n, 0]
        lhs_v[2 * n : 2 * n + 2, 128:256] = recv2[n, 1]
    lhs = lhs_v[...].astype(BF16)
    for n in range(6):
        low = slice(256 * n, 256 * n + 256)
        high = slice(1536 + 256 * n, 1536 + 256 * n + 256)
        pa = jnp.dot(lhs, wo_v[:, low], preferred_element_type=F32) + acc_v[:, low]
        pb = jnp.dot(lhs, wo_v[:, high], preferred_element_type=F32) + acc_v[:, high]
        turned = jnp.concatenate([pa, pb], axis=0).T.astype(BF16)
        for w in range(16):
            at = 256 * n + 16 * w
            zl, rest = divmod(at, 768)
            dd, e = divmod(rest, 48)
            p1send[zl, dd, e : e + 16, :] = turned[16 * w : 16 * w + 16]

    def scatter(n, carry):
        @pl.when(n != d16)
        def _():
            pltpu.make_async_remote_copy(
                src_ref=p1send.at[:, n],
                dst_ref=recvp1.at[d16],
                send_sem=sp1,
                recv_sem=rp1,
                device_id=(s, 8 * z + n // 2, n % 2),
                device_id_type=MESH,
            ).start()

        return carry

    lax.fori_loop(0, 16, scatter, 0)
    recvp1[d16] = p1send[:, d16]
    most1 = recvp1.at[pl.ds(0, 15)]
    wait_recv(most1, most1, sp1, rp1)
    lane24 = lax.broadcasted_iota(jnp.int32, (24, 128), 1) < 64
    for cs in range(2):
        for zl in range(2):
            part = recvp1[cs, zl].astype(F32)
            for p in range(1, 8):
                part = part + recvp1[2 * p + cs, zl].astype(F32)
            a, b = part[0:24], part[24:48]
            p2send[4 * cs + zl] = jnp.where(lane24, a, pltpu.roll(b, 64, 1)).astype(BF16)
            p2send[4 * cs + 2 + zl] = jnp.where(lane24, pltpu.roll(a, 64, 1), b).astype(BF16)

    def along(n, carry):
        @pl.when(n != z)
        def _():
            pltpu.make_async_remote_copy(
                src_ref=p2send.at[n],
                dst_ref=recvp2.at[z],
                send_sem=sp2,
                recv_sem=rp2,
                device_id=(s, 8 * n + chip, c),
                device_id_type=MESH,
            ).start()

        return carry

    lax.fori_loop(0, 8, along, 0)
    recvp2[z] = p2send[z]
    most2 = recvp2.at[pl.ds(0, 7)]
    wait_recv(most2, most2, sp2, rp2)
    last = recvp2[0].astype(F32)
    for n in range(1, 8):
        last = last + recvp2[n].astype(F32)
    result = jnp.concatenate([last, pltpu.roll(last, 64, 1)], axis=0)[:, 0:64]
    out[...] = (result + res_v[pl.ds(res_off, 48), :]).astype(BF16)

    edge = (t == 0) | (t == 7)
    for count, when in (
        (64, jnp.logical_not(edge) & jnp.logical_not(mine)),
        (63, jnp.logical_not(edge) & mine),
        (32, edge & jnp.logical_not(mine)),
        (31, edge & mine),
    ):

        @pl.when(when)
        def _():
            part = send1.at[pl.ds(0, count)]
            wait_send(part, part, s1, r1)

    wait_send(most, most, s2, r2)
    wait_send(most1, most1, sp1, rp1)
    wait_send(most2, most2, sp2, rp2)


def body(
    hidden, gain, qkv, out_w, gate, up, down, keys, values, positions, write_slots
):
    half = THETA ** (-2.0 * np.arange(64) / HD)
    freq = jnp.asarray(np.concatenate([half, half])[None, :].astype(np.float32))
    hbm = pl.BlockSpec(memory_space=pl.ANY)
    vmem = pl.BlockSpec(memory_space=pltpu.VMEM)
    smem = pl.BlockSpec(memory_space=pltpu.SMEM)
    dma = pltpu.SemaphoreType.DMA
    V = pltpu.VMEM
    result = pl.pallas_call(
        kernel,
        out_shape=jax.ShapeDtypeStruct((48, 64), BF16),
        in_specs=[hbm] * 9 + [smem, smem, vmem],
        out_specs=vmem,
        scratch_shapes=[
            V((64, D), BF16),
            V((96, 128), F32),
            V((128, HALF), BF16),
            V((256, NCOL), BF16),
            V((FFB, HALF), BF16),
            V((FFB, HALF), BF16),
            V((2, FFB, NCOL), BF16),
            V((2, WIN, HD), BF16),
            V((2, WIN, HD), BF16),
            V((64, HALF), BF16),
            V((64, 2, 128), F32),
            V((56, 2, 128), F32),
            V((2, 16, 128), F32),
            V((8, 128), F32),
            V((12, 2, 128), F32),
            V((32, 2, 2, 128), F32),
            V((64, 256), F32),
            V((FFB, 128), F32),
            V((FFB, 128), F32),
            V((2, FFB, 128), BF16),
            V((64, NCOL), F32),
            V((2, 16, 48, 128), BF16),
            V((16, 2, 48, 128), BF16),
            V((8, 24, 128), BF16),
            V((8, 24, 128), BF16),
            V((256, 64), F32),
            dma((9,)),
            dma, dma,
            dma((2,)), dma((2,)),
            dma, dma, dma, dma, dma, dma, dma, dma, dma, dma,
        ],
        compiler_params=pltpu.CompilerParams(
            collective_id=0, has_side_effects=True, vmem_limit_bytes=60 * 1024 * 1024
        ),
        name="layer",
    )(
        hidden,
        gain.reshape(96, 128),
        qkv.T,
        out_w,
        gate.T,
        up.T,
        down,
        keys,
        values,
        positions,
        write_slots,
        freq,
    )
    return result.T


def solution(mesh):
    side, grp, rep = mesh.axis_names
    inner = (grp, rep)
    every = (side, grp, rep)
    placed = (
        P(),
        P(),
        P(side, inner),
        P(inner, side),
        P(side, inner),
        P(side, inner),
        P(inner, side),
        P(every, None, None),
        P(every, None, None),
        P(),
        P(),
    )
    return jax.shard_map(
        body, mesh=mesh, in_specs=placed, out_specs=P(None, every), check_vma=False
    )
```

time: 157 us -> 44.7 us (0.28); the launches traced: 155 us -> 44.3 us
  Pallas kernels: 0 us -> 43 us
  waiting for transfers between devices: 39.7 us -> 0 us
  starting transfers between devices: 33.2 us -> 0 us
  local copies, waits for them, and re-layouts: 27.3 us -> 1.31 us
  other arithmetic: 19.9 us -> 0 us
  blocking collectives: 19 us -> 0 us
  matrix products: 15 us -> 0 us
    pallas_call x0 -> x1, Pallas kernels: none -> 43 us  [body(): pl.pallas_call(kernel, out_shape=jax.ShapeDtypeStruct((48, 64), BF16), in...]
    all_to_all x4 -> x0, waiting for transfers between devices: 37.3 us -> none  [the longest x1 20.1 us: sum_in_two_steps(): return jnp.sum(lax.all_to_all(own, far, 0, 0, tiled=True), axis=0)]
    all_to_all x4 -> x0, starting transfers between devices: 26.2 us -> none  [the longest x2 15.2 us: copy_for_each(): lax.all_to_all(jnp.broadcast_to(array[None], (size, *array.shape)), axis,...]
    all_to_all x2 -> x0, blocking collectives: 19 us -> none  [the longest x1 9.92 us: sent_and_summed(): lax.all_to_all(tiles, axis, split_axis=0, concat_axis=0, tiled=True)]
    unnamed x23 -> x1, local copies, waits for them, and re-layouts: 13.7 us -> 1.31 us
    dot_general x6 -> x0, matrix products: 11.9 us -> none  [the longest x1 3.55 us: attend(): jnp.einsum('tpj,tjd->tpd', probs, values_now, preferred_element_type=jnp....]
    all_to_all x2 -> x0, other arithmetic: 10.2 us -> none  [the longest x1 6.61 us: sent_and_summed(): lax.all_to_all(tiles, axis, split_axis=0, concat_axis=0, tiled=True)]
    ppermute x5 -> x0, starting transfers between devices: 7.04 us -> none  [from_partner(): return lax.ppermute(value, axis, pairs)]
  transfers between devices with their start and end apart: 9 -> 0, of which waited for: 6 -> 0; matrix products, arithmetic and copies ran while one was open for 5% -> 0% of each run, Pallas kernels for 0% -> 0%
where the time goes in v1:
time: 44.7 us; the launch traced here: 44.3 us
  Pallas kernels  43 us (96%)
  local copies, waits for them, and re-layouts  1.31 us (3%)
    pallas_call x1, Pallas kernels, body(): pl.pallas_call(kernel, out_shape=jax.ShapeDtypeStruct((48, 64), BF16), in...  43 us
    unnamed x1, local copies, waits for them, and re-layouts  1.31 us

profile of v1, /device:TPU:1, one launch (start us, length us, event | category | flops | bytes accessed | tf_op | source)
XLA Modules:
  0.0 44.3 jit_solution(1455721381423282787)
XLA Ops:
  0.0 43.0 %layer.1 = bf16[48,64]{1,0:T(8,128)(2,1)} custom-call(bf16[64,12288]{1,0:T(8,128)(2,1)} %hidden.1, f32[96,128]{1,0:T(8,128)} %bitcast.8, bf16[112,6144]{1,0:T(8,128)(2,1)} %bitcast.7, bf16[96,6144]{1,0:T(8,128)(2,1)} %out_w.1, bf16[136,6144]{1,0:T(8,128)(2,1)} %bitcast.5, bf16[136,6144]{1,0:T(8,128)(2,1)} %bitcast.6, bf16[136,6144]{1,0:T(8,128)(2,1)} %down.1, ...), custom_call_target="tpu_custom_call" | custom-call | tf_op jit(solution)/shard_map/layer/pallas_call | solution.py:410
  43.0 1.3 %copy.14 = bf16[64,48]{0,1:T(8,128)(2,1)} copy(bf16[64,48]{0,1:T(8,128)(2,1)} %bitcast.9) | data formatting | bytes 12288

commit v2 on v1

--- a/solution.py
+++ b/solution.py
@@ -23,70 +23,106 @@
 SCALE = 1.0 / math.sqrt(HD)
 F32 = jnp.float32
 BF16 = jnp.bfloat16
+
+
+def div(a, b):
+    return lax.div(a, jnp.int32(b))
+
+
+def rem(a, b):
+    return lax.rem(a, jnp.int32(b))
+
+
 NT = (((1,), (1,)), ((), ()))
 TN = (((0,), (0,)), ((), ()))
 
 
 def kernel(
-    hidden, gain, qkv, out_w, gate, up, down, keys, values, pos, slots, freq, out,
+    hidden, gain, qkv, out_w, gate, up, down, keys, values, pos_h, slots_h, freq_h, out,
     hid_v, gain_v, qkv_v, wo_v, gate_v, up_v, wd_v, k_v, v_v, normed_v,
     send1, recv1, qrow, cs_v, att_v, recv2, lhs_v, gu_send, gu_recv, act_v, acc_v,
-    p1send, recvp1, p2send, recvp2, res_v,
+    p1send, recvp1, p2send, recvp2, res_v, pos, slots, freq,
     load_sem, s1, r1, spre, rpre, s2, r2, s3, r3, s4, r4, sp1, rp1, sp2, rp2,
 ):
     s = lax.axis_index("side")
     g = lax.axis_index("grp")
     c = lax.axis_index("rep")
-    z = g // 8
-    chip = g % 8
+    z = div(g, 8)
+    chip = rem(g, 8)
     j = 2 * g + c
     d16 = 2 * chip + c
-    row_off = 64 * (chip % 2)
+    row_off = 64 * (rem(chip, 2))
 
     def load(src, dst, n):
         cp = pltpu.make_async_copy(src, dst, load_sem.at[n])
         cp.start()
         return cp
 
-    hid_cp = load(hidden, hid_v, 0)
-    gain_cp = load(gain, gain_v, 1)
-    qkv_cp = load(qkv, qkv_v.at[pl.ds(0, COLS)], 2)
-    gate_cp = load(gate, gate_v, 3)
-    up_cp = load(up, up_v, 4)
-    k_cp = load(keys, k_v, 5)
-    v_cp = load(values, v_v, 6)
+    quarter = D // 4
+    hid_cp = [
+        load(
+            hidden.at[:, pl.ds(quarter * n, quarter)],
+            hid_v.at[:, pl.ds(quarter * n, quarter)],
+            n,
+        )
+        for n in range(4)
+    ]
+    gain_cp = load(gain, gain_v, 4)
+    qkv_cp = load(qkv, qkv_v.at[pl.ds(0, COLS)], 5)
+
+    barrier = pltpu.get_barrier_semaphore()
+
+    def greet(side, grp, rep):
+        pl.semaphore_signal(
+            barrier, inc=1, device_id=(side, grp, rep), device_id_type=MESH
+        )
+
+    source = 8 * div(z, 7) + rem(z, 7)
+    left = rem(z, 7)
+    for cc in range(14):
+        for near in (source, source + 1):
+            greet(1 - s, div(near, 2), rem(near, 2))
+
+            @pl.when(near != j)
+            def _():
+                greet(s, div(near, 2), rem(near, 2))
+
+        left = left + 1
+        wrap = left == 7
+        source = source + jnp.where(wrap, 10, 9)
+        left = jnp.where(wrap, 0, left)
+    for o in range(16):
+        i = rem(d16 + o, 16)
+        greet(1 - s, 8 * z + div(i, 2), rem(i, 2))
+        if o > 0:
+            greet(s, 8 * z + div(i, 2), rem(i, 2))
+    for o in range(1, 8):
+        greet(s, 8 * rem(z + o, 8) + chip, c)
+
+    gate_cp = load(gate, gate_v, 6)
+    up_cp = load(up, up_v, 7)
+    k_cp = load(keys, k_v, 8)
+    v_cp = load(values, v_v, 9)
     own_cols = pl.ds(pl.multiple_of(NCOL * c, NCOL), NCOL)
     wo_cp = load(
-        out_w.at[:, own_cols], wo_v.at[pl.ds(pl.multiple_of(row_off + OB * c, 32), OB)], 7
-    )
-    wd_cp = load(down.at[:, own_cols], wd_v.at[c], 8)
-
-    barrier = pltpu.get_barrier_semaphore()
-
-    def greet(n, carry):
-        b, rest = n // 128, n % 128
-
-        @pl.when(jnp.logical_not((b == s) & (rest == j)))
-        def _():
-            pl.semaphore_signal(
-                barrier, inc=1, device_id=(b, rest // 2, rest % 2), device_id_type=MESH
-            )
-
-        return carry
-
-    lax.fori_loop(0, 256, greet, 0)
+        out_w.at[:, own_cols], wo_v.at[pl.ds(pl.multiple_of(row_off + OB * c, 32), OB)], 10
+    )
+    wd_cp = load(down.at[:, own_cols], wd_v.at[c], 11)
+    pos_cp = load(pos_h, pos, 12)
+    slots_cp = load(slots_h, slots, 13)
+    freq_cp = load(freq_h, freq, 14)
 
     qkv_v[pl.ds(COLS, 16), :] = jnp.zeros((16, HALF), BF16)
-    wo_v[pl.ds(pl.multiple_of(192 - 192 * (chip % 2), 64), 64), :] = jnp.zeros((64, NCOL), BF16)
-
-    hid_cp.wait()
+    wo_v[pl.ds(pl.multiple_of(192 - 192 * (rem(chip, 2)), 64), 64), :] = jnp.zeros((64, NCOL), BF16)
+
 
     def chunk(i):
         return hid_v[:, pl.ds(pl.multiple_of(i * 128, 128), 128)].astype(F32)
 
-    total = lax.fori_loop(
-        0, 96, lambda i, a: a + chunk(i), jnp.zeros((64, 128), F32), unroll=8
-    )
+    total = jnp.zeros((64, 128), F32)
+    for n in range(4):
+        hid_cp[n].wait()
+        total = lax.fori_loop(24 * n, 24 * n + 24, lambda i, a: a + chunk(i), total, unroll=8)
     mean = jnp.sum(total, axis=1, keepdims=True) * (1.0 / D)
 
     def square(i, a):
@@ -108,7 +144,7 @@
 
     qkv_cp.wait()
     term = lax.dot_general(normed_v[...], qkv_v[...], NT, preferred_element_type=F32)
-    m, t = j // 8, j % 8
+    m, t = div(j, 8), rem(j, 8)
     rolled = pltpu.roll(term, (128 - 16 * t) % 128, 1)
     lane = lax.broadcasted_iota(jnp.int32, (64, 128), 1)
     first = jnp.where(lane < COLS - 16 * t, rolled, 0.0)
@@ -117,34 +153,37 @@
         send1[n] = first[2 * n : 2 * n + 2]
         send1[32 + n] = second[2 * n : 2 * n + 2]
 
-    pl.semaphore_wait(barrier, 255)
+    mine = ((t <= 6) & (rem(7 * m + t, 8) == z)) | ((t >= 1) & (rem(7 * m + t + 7, 8) == z))
+    edge = (t == 0) | (t == 7)
+    pl.semaphore_wait(barrier, jnp.where(edge, 70, 102) - jnp.where(mine, 1, 0))
 
     valid = (t <= 6, t >= 1)
     for piece in range(2):
         q = jnp.maximum(7 * m + t - piece, 0)
-        k, cc = q % 8, q // 8
+        k, cc = rem(q, 8), div(q, 8)
         slot = jnp.minimum(cc, 13) * 4 + piece * 2 + s
 
         @pl.when(valid[piece])
         def _():
-            def push(n, carry):
-                b, i = n // 16, n % 16
-                there = 8 * k + i // 2
-
-                @pl.when(jnp.logical_not((b == s) & (there == g) & (i % 2 == c)))
-                def _():
-                    pltpu.make_async_remote_copy(
-                        src_ref=send1.at[32 * piece + n],
-                        dst_ref=recv1.at[slot],
-                        send_sem=s1,
-                        recv_sem=r1,
-                        device_id=(b, there, i % 2),
-                        device_id_type=MESH,
-                    ).start()
-
-                return carry
-
-            lax.fori_loop(0, 32, push, 0)
+            def push(b, i):
+                pltpu.make_async_remote_copy(
+                    src_ref=send1.at[32 * piece + 16 * b + i],
+                    dst_ref=recv1.at[slot],
+                    send_sem=s1,
+                    recv_sem=r1,
+                    device_id=(b, 8 * k + div(i, 2), rem(i, 2)),
+                    device_id_type=MESH,
+                ).start()
+
+            for o in range(16):
+                i = rem(d16 + o, 16)
+                push(1 - s, i)
+                if o > 0:
+                    push(s, i)
+
+            @pl.when(k != z)
+            def _():
+                push(s, d16)
 
             @pl.when(k == z)
             def _():
@@ -190,20 +229,21 @@
     gu.start()
 
     col0 = 48 * (128 * s + j)
-    tile = jnp.minimum(col0 // 128, 94)
+    tile = jnp.minimum(div(col0, 128), 94)
     res_v[...] = hid_v[:, pl.ds(pl.multiple_of(tile * 128, 128), 256)].astype(F32).T
     res_off = pl.multiple_of(col0 - tile * 128, 16)
 
     lane1 = lax.broadcasted_iota(jnp.int32, (1, 128), 1)
     row0 = 32 * s + 2 * d16
+    pos_cp.wait()
+    slots_cp.wait()
+    freq_cp.wait()
     for r in range(2):
         angle = pos[row0 + r].astype(F32) * freq[...]
         sine = jnp.sin(angle)
         cs_v[2 * r : 2 * r + 1, :] = jnp.cos(angle)
         cs_v[2 * r + 1 : 2 * r + 2, :] = jnp.where(lane1 < 64, -sine, sine)
     qrow[...] = jnp.zeros((2, 16, 128), F32)
-
-    mine = ((t <= 6) & ((7 * m + t) % 8 == z)) | ((t >= 1) & ((7 * m + t + 7) % 8 == z))
 
     def wait_recv(src, dst, send, recv):
         pltpu.make_async_remote_copy(
@@ -262,25 +302,23 @@
 
     here = s * 16 + d16
 
-    def spread_heads(n, carry):
-        b, i = n // 16, n % 16
-        u = i // 2
-
-        @pl.when(jnp.logical_not((b == s) & (i == d16)))
-        def _():
-            pltpu.make_async_remote_copy(
-                src_ref=att_v.at[pl.ds(3 * u // 2, 2)],
-                dst_ref=recv2.at[here],
-                send_sem=s2,
-                recv_sem=r2,
-                device_id=(b, 8 * z + u, i % 2),
-                device_id_type=MESH,
-            ).start()
-
-        return carry
-
-    lax.fori_loop(0, 32, spread_heads, 0)
-    recv2[here] = att_v[pl.ds(3 * chip // 2, 2)]
+    def spread_heads(b, i):
+        u = div(i, 2)
+        pltpu.make_async_remote_copy(
+            src_ref=att_v.at[pl.ds(div(3 * u, 2), 2)],
+            dst_ref=recv2.at[here],
+            send_sem=s2,
+            recv_sem=r2,
+            device_id=(b, 8 * z + u, rem(i, 2)),
+            device_id_type=MESH,
+        ).start()
+
+    for o in range(16):
+        i = rem(d16 + o, 16)
+        spread_heads(1 - s, i)
+        if o > 0:
+            spread_heads(s, i)
+    recv2[here] = att_v[pl.ds(div(3 * chip, 2), 2)]
 
     gu.wait()
     both = gu_send[...] + gu_recv[...]
@@ -327,21 +365,16 @@
             dd, e = divmod(rest, 48)
             p1send[zl, dd, e : e + 16, :] = turned[16 * w : 16 * w + 16]
 
-    def scatter(n, carry):
-        @pl.when(n != d16)
-        def _():
-            pltpu.make_async_remote_copy(
-                src_ref=p1send.at[:, n],
-                dst_ref=recvp1.at[d16],
-                send_sem=sp1,
-                recv_sem=rp1,
-                device_id=(s, 8 * z + n // 2, n % 2),
-                device_id_type=MESH,
-            ).start()
-
-        return carry
-
-    lax.fori_loop(0, 16, scatter, 0)
+    for o in range(1, 16):
+        n = rem(d16 + o, 16)
+        pltpu.make_async_remote_copy(
+            src_ref=p1send.at[:, n],
+            dst_ref=recvp1.at[d16],
+            send_sem=sp1,
+            recv_sem=rp1,
+            device_id=(s, 8 * z + div(n, 2), rem(n, 2)),
+            device_id_type=MESH,
+        ).start()
     recvp1[d16] = p1send[:, d16]
     most1 = recvp1.at[pl.ds(0, 15)]
     wait_recv(most1, most1, sp1, rp1)
@@ -355,21 +388,16 @@
             p2send[4 * cs + zl] = jnp.where(lane24, a, pltpu.roll(b, 64, 1)).astype(BF16)
             p2send[4 * cs + 2 + zl] = jnp.where(lane24, pltpu.roll(a, 64, 1), b).astype(BF16)
 
-    def along(n, carry):
-        @pl.when(n != z)
-        def _():
-            pltpu.make_async_remote_copy(
-                src_ref=p2send.at[n],
-                dst_ref=recvp2.at[z],
-                send_sem=sp2,
-                recv_sem=rp2,
-                device_id=(s, 8 * n + chip, c),
-                device_id_type=MESH,
-            ).start()
-
-        return carry
-
-    lax.fori_loop(0, 8, along, 0)
+    for o in range(1, 8):
+        n = rem(z + o, 8)
+        pltpu.make_async_remote_copy(
+            src_ref=p2send.at[n],
+            dst_ref=recvp2.at[z],
+            send_sem=sp2,
+            recv_sem=rp2,
+            device_id=(s, 8 * n + chip, c),
+            device_id_type=MESH,
+        ).start()
     recvp2[z] = p2send[z]
     most2 = recvp2.at[pl.ds(0, 7)]
     wait_recv(most2, most2, sp2, rp2)
@@ -379,7 +407,6 @@
     result = jnp.concatenate([last, pltpu.roll(last, 64, 1)], axis=0)[:, 0:64]
     out[...] = (result + res_v[pl.ds(res_off, 48), :]).astype(BF16)
 
-    edge = (t == 0) | (t == 7)
     for count, when in (
         (64, jnp.logical_not(edge) & jnp.logical_not(mine)),
         (63, jnp.logical_not(edge) & mine),
@@ -404,13 +431,12 @@
     freq = jnp.asarray(np.concatenate([half, half])[None, :].astype(np.float32))
     hbm = pl.BlockSpec(memory_space=pl.ANY)
     vmem = pl.BlockSpec(memory_space=pltpu.VMEM)
-    smem = pl.BlockSpec(memory_space=pltpu.SMEM)
     dma = pltpu.SemaphoreType.DMA
     V = pltpu.VMEM
     result = pl.pallas_call(
         kernel,
         out_shape=jax.ShapeDtypeStruct((48, 64), BF16),
-        in_specs=[hbm] * 9 + [smem, smem, vmem],
+        in_specs=[hbm] * 12,
         out_specs=vmem,
         scratch_shapes=[
             V((64, D), BF16),
@@ -439,7 +465,10 @@
             V((8, 24, 128), BF16),
             V((8, 24, 128), BF16),
             V((256, 64), F32),
-            dma((9,)),
+            pltpu.SMEM((64,), jnp.int32),
+            pltpu.SMEM((64,), jnp.int32),
+            V((1, 128), F32),
+            dma((15,)),
             dma, dma,
             dma((2,)), dma((2,)),
             dma, dma, dma, dma, dma, dma, dma, dma, dma, dma,

time: 44.7 us -> 40.3 us (0.902)
  Pallas kernels: 43 us -> 38.8 us
    pallas_call x1, Pallas kernels: 43 us -> 38.8 us  [body(): pl.pallas_call(kernel, out_shape=jax.ShapeDtypeStruct((48, 64), BF16), in...]
where the time goes in v2:
time: 40.3 us; the launch traced here: 40.1 us
  Pallas kernels  38.8 us (96%)
  local copies, waits for them, and re-layouts  1.31 us (3%)
    pallas_call x1, Pallas kernels, body(): pl.pallas_call(kernel, out_shape=jax.ShapeDtypeStruct((48, 64), BF16), in...  38.8 us
    unnamed x1, local copies, waits for them, and re-layouts  1.31 us

profile of v2, /device:TPU:1, one launch (start us, length us, event | category | flops | bytes accessed | tf_op | source)
XLA Modules:
  0.0 40.1 jit_solution(17648315675410570273)
XLA Ops:
  0.0 38.8 %layer.1 = bf16[48,64]{1,0:T(8,128)(2,1)} custom-call(bf16[64,12288]{1,0:T(8,128)(2,1)} %hidden.1, f32[96,128]{1,0:T(8,128)} %bitcast.8, bf16[112,6144]{1,0:T(8,128)(2,1)} %bitcast.7, bf16[96,6144]{1,0:T(8,128)(2,1)} %out_w.1, bf16[136,6144]{1,0:T(8,128)(2,1)} %bitcast.5, bf16[136,6144]{1,0:T(8,128)(2,1)} %bitcast.6, bf16[136,6144]{1,0:T(8,128)(2,1)} %down.1, ...), custom_call_target="tpu_custom_call" | custom-call | tf_op jit(solution)/shard_map/layer/pallas_call | solution.py:436
  38.8 1.3 %copy.14 = bf16[64,48]{0,1:T(8,128)(2,1)} copy(bf16[64,48]{0,1:T(8,128)(2,1)} %bitcast.9) | data formatting | bytes 12288

commit v3 on v2

--- a/solution.py
+++ b/solution.py
@@ -119,31 +119,36 @@
     def chunk(i):
         return hid_v[:, pl.ds(pl.multiple_of(i * 128, 128), 128)].astype(F32)
 
-    total = jnp.zeros((64, 128), F32)
+    hid_cp[0].wait()
+    pivot = jnp.sum(chunk(0), axis=1, keepdims=True) * (1.0 / 128)
+
+    def moments(i, carry):
+        one, two = carry
+        d = chunk(i) - pivot
+        return one + d, two + d * d
+
+    carry = (jnp.zeros((64, 128), F32), jnp.zeros((64, 128), F32))
     for n in range(4):
-        hid_cp[n].wait()
-        total = lax.fori_loop(24 * n, 24 * n + 24, lambda i, a: a + chunk(i), total, unroll=8)
-    mean = jnp.sum(total, axis=1, keepdims=True) * (1.0 / D)
-
-    def square(i, a):
-        d = chunk(i) - mean
-        return a + d * d
-
-    spread = lax.fori_loop(0, 96, square, jnp.zeros((64, 128), F32), unroll=8)
-    var = jnp.sum(spread, axis=1, keepdims=True) * (1.0 / D)
-    rstd = lax.rsqrt(var + EPSILON)
+        if n > 0:
+            hid_cp[n].wait()
+        carry = lax.fori_loop(24 * n, 24 * n + 24, moments, carry, unroll=8)
+    shift = jnp.sum(carry[0], axis=1, keepdims=True) * (1.0 / D)
+    mean = pivot + shift
+    var = jnp.sum(carry[1], axis=1, keepdims=True) * (1.0 / D) - shift * shift
+    rstd = lax.rsqrt(jnp.maximum(var, 0.0) + EPSILON)
     gain_cp.wait()
-
-    def norm(i, carry):
-        n = s * 48 + i
-        v = (chunk(n) - mean) * rstd * gain_v[pl.ds(n, 1), :]
-        normed_v[:, pl.ds(pl.multiple_of(i * 128, 128), 128)] = v.astype(BF16)
-        return carry
-
-    lax.fori_loop(0, 48, norm, 0, unroll=4)
-
     qkv_cp.wait()
-    term = lax.dot_general(normed_v[...], qkv_v[...], NT, preferred_element_type=F32)
+
+    term = jnp.zeros((64, 128), F32)
+    for n in range(12):
+        for w in range(4):
+            at = 4 * n + w
+            v = (chunk(s * 48 + at) - mean) * rstd * gain_v[pl.ds(s * 48 + at, 1), :]
+            normed_v[:, 128 * at : 128 * at + 128] = v.astype(BF16)
+        cols = slice(512 * n, 512 * n + 512)
+        term = term + lax.dot_general(
+            normed_v[:, cols], qkv_v[:, cols], NT, preferred_element_type=F32
+        )
     m, t = div(j, 8), rem(j, 8)
     rolled = pltpu.roll(term, (128 - 16 * t) % 128, 1)
     lane = lax.broadcasted_iota(jnp.int32, (64, 128), 1)
@@ -353,6 +358,18 @@
         lhs_v[2 * n : 2 * n + 2, 0:128] = recv2[n, 0]
         lhs_v[2 * n : 2 * n + 2, 128:256] = recv2[n, 1]
     lhs = lhs_v[...].astype(BF16)
+    def scatter(zl):
+        for o in range(1, 16):
+            n = rem(d16 + o, 16)
+            pltpu.make_async_remote_copy(
+                src_ref=p1send.at[zl, n],
+                dst_ref=recvp1.at[d16, zl],
+                send_sem=sp1,
+                recv_sem=rp1,
+                device_id=(s, 8 * z + div(n, 2), rem(n, 2)),
+                device_id_type=MESH,
+            ).start()
+
     for n in range(6):
         low = slice(256 * n, 256 * n + 256)
         high = slice(1536 + 256 * n, 1536 + 256 * n + 256)
@@ -365,16 +382,8 @@
             dd, e = divmod(rest, 48)
             p1send[zl, dd, e : e + 16, :] = turned[16 * w : 16 * w + 16]
 
-    for o in range(1, 16):
-        n = rem(d16 + o, 16)
-        pltpu.make_async_remote_copy(
-            src_ref=p1send.at[:, n],
-            dst_ref=recvp1.at[d16],
-            send_sem=sp1,
-            recv_sem=rp1,
-            device_id=(s, 8 * z + div(n, 2), rem(n, 2)),
-            device_id_type=MESH,
-        ).start()
+    scatter(0)
+    scatter(1)
     recvp1[d16] = p1send[:, d16]
     most1 = recvp1.at[pl.ds(0, 15)]
     wait_recv(most1, most1, sp1, rp1)
@@ -435,7 +444,7 @@
     V = pltpu.VMEM
     result = pl.pallas_call(
         kernel,
-        out_shape=jax.ShapeDtypeStruct((48, 64), BF16),
+        out_shape=pltpu.VMEM((48, 64), BF16),
         in_specs=[hbm] * 12,
         out_specs=vmem,
         scratch_shapes=[

time: 40.3 us -> 39.1 us (0.970)
  local copies, waits for them, and re-layouts: 1.31 us -> 0.6 us
    unnamed x1, local copies, waits for them, and re-layouts: 1.31 us -> 0.6 us
    pallas_call x1, Pallas kernels: 38.8 us -> 38.4 us  [body(): pl.pallas_call(kernel, out_shape=pltpu.VMEM((48, 64), BF16), in_specs=[hb...]
where the time goes in v3:
time: 39.1 us; the launch traced here: 39 us
  Pallas kernels  38.4 us (98%)
  local copies, waits for them, and re-layouts  0.6 us (2%)
    pallas_call x1, Pallas kernels, body(): pl.pallas_call(kernel, out_shape=pltpu.VMEM((48, 64), BF16), in_specs=[hb...  38.4 us

profile of v3, /device:TPU:1, one launch (start us, length us, event | category | flops | bytes accessed | tf_op | source)
XLA Modules:
  0.0 39.0 jit_solution(4896796897713671529)
XLA Ops:
  0.0 38.4 %layer.1 = bf16[48,64]{1,0:T(8,128)(2,1)S(1)} custom-call(bf16[64,12288]{1,0:T(8,128)(2,1)} %hidden.1, f32[96,128]{1,0:T(8,128)} %bitcast.9, bf16[112,6144]{1,0:T(8,128)(2,1)} %bitcast.8, bf16[96,6144]{1,0:T(8,128)(2,1)} %out_w.1, bf16[136,6144]{1,0:T(8,128)(2,1)} %bitcast.6, bf16[136,6144]{1,0:T(8,128)(2,1)} %bitcast.7, bf16[136,6144]{1,0:T(8,128)(2,1)} %down.1, ...), custom_call_target="tpu_custom_call" | custom-call | tf_op jit(solution)/shard_map/layer/pallas_call | solution.py:445
  38.4 0.6 %copy.14 = bf16[64,48]{0,1:T(8,128)(2,1)} copy(bf16[64,48]{0,1:T(8,128)(2,1)S(1)} %bitcast.5) | data formatting | bytes 12288

commit v4 on v3

--- a/solution.py
+++ b/solution.py
@@ -20,7 +20,7 @@
 FFB = 136
 OB = 96
 NCOL = 3072
-SCALE = 1.0 / math.sqrt(HD)
+SCALE2 = 1.0 / math.sqrt(HD) / math.log(2.0)
 F32 = jnp.float32
 BF16 = jnp.bfloat16
 
@@ -41,8 +41,8 @@
     hidden, gain, qkv, out_w, gate, up, down, keys, values, pos_h, slots_h, freq_h, out,
     hid_v, gain_v, qkv_v, wo_v, gate_v, up_v, wd_v, k_v, v_v, normed_v,
     send1, recv1, qrow, cs_v, att_v, recv2, lhs_v, gu_send, gu_recv, act_v, acc_v,
-    p1send, recvp1, p2send, recvp2, res_v, pos, slots, freq,
-    load_sem, s1, r1, spre, rpre, s2, r2, s3, r3, s4, r4, sp1, rp1, sp2, rp2,
+    p1send, recvp1, p2send, recvp2, res_v, pos, slots, freq, bias_v, zsend, zrecv, zsum,
+    load_sem, s1, r1, spre, rpre, s2, r2, s3, r3, s4, r4, sp1, rp1, sp2, rp2, sz, rz, sz2,
 ):
     s = lax.axis_index("side")
     g = lax.axis_index("grp")
@@ -52,6 +52,10 @@
     j = 2 * g + c
     d16 = 2 * chip + c
     row_off = 64 * (rem(chip, 2))
+    x, y = rem(chip, 4), div(chip, 4)
+    odd = rem(x + y, 2)
+    is_plane = (c == 0) | (odd == 1)
+    is_line = c == div(z, 4)
 
     def load(src, dst, n):
         cp = pltpu.make_async_copy(src, dst, load_sem.at[n])
@@ -249,6 +253,10 @@
         cs_v[2 * r : 2 * r + 1, :] = jnp.cos(angle)
         cs_v[2 * r + 1 : 2 * r + 2, :] = jnp.where(lane1 < 64, -sine, sine)
     qrow[...] = jnp.zeros((2, 16, 128), F32)
+    column = lax.broadcasted_iota(jnp.int32, (8, WIN), 1)
+    for r in range(2):
+        age = (slots[row0 + r] - column) & (WIN - 1)
+        bias_v[r] = jnp.where((age > 0) & (age <= pos[row0 + r]), 0.0, MASKED)
 
     def wait_recv(src, dst, send, recv):
         pltpu.make_async_remote_copy(
@@ -279,28 +287,23 @@
 
     k_cp.wait()
     v_cp.wait()
-    column = lax.broadcasted_iota(jnp.int32, (16, WIN), 1)
     for r in range(2):
-        x = qrow[r]
-        turned = x * cs_v[2 * r : 2 * r + 1, :] + pltpu.roll(x, 64, 1) * cs_v[2 * r + 1 : 2 * r + 2, :]
+        heads = qrow[r]
+        turned = heads * cs_v[2 * r : 2 * r + 1, :] + pltpu.roll(heads, 64, 1) * cs_v[2 * r + 1 : 2 * r + 2, :]
         query = turned.astype(BF16)
         rounded = query.astype(F32)
         new_key = rounded[12:13]
-        new_value = x[13:14]
-        slot_r = slots[row0 + r]
-        pos_r = pos[row0 + r]
-        hit = column == slot_r
-        fresh = jnp.sum(rounded * new_key, axis=1, keepdims=True) * SCALE
-        scores = lax.dot_general(query, k_v[r], NT, preferred_element_type=F32) * SCALE
-        scores = jnp.where(hit, fresh, scores)
-        usable = ((slot_r - column) & (WIN - 1)) <= pos_r
-        scores = jnp.where(usable, scores, MASKED)
-        highest = jnp.max(scores, axis=1, keepdims=True)
-        weights = jnp.exp(scores - highest)
-        denom = jnp.sum(weights, axis=1, keepdims=True)
-        stale = jnp.where(hit, 0.0, weights).astype(BF16)
-        summed = jnp.dot(stale, v_v[r], preferred_element_type=F32)
-        own = jnp.exp(fresh - highest).astype(BF16).astype(F32)
+        new_value = heads[13:14]
+        fresh = jnp.sum(rounded * new_key, axis=1, keepdims=True)
+        bias = bias_v[r]
+        scores = lax.dot_general(query, k_v[r], NT, preferred_element_type=F32)
+        scores = scores + jnp.concatenate([bias, bias], axis=0)
+        highest = jnp.maximum(jnp.max(scores, axis=1, keepdims=True), fresh)
+        weights = jnp.exp2((scores - highest) * SCALE2)
+        own = jnp.exp2((fresh - highest) * SCALE2)
+        denom = jnp.sum(weights, axis=1, keepdims=True) + own
+        summed = jnp.dot(weights.astype(BF16), v_v[r], preferred_element_type=F32)
+        own = own.astype(BF16).astype(F32)
         attended = ((summed + own * new_value) / denom).astype(BF16).astype(F32)
         for h in range(12):
             att_v[h, r : r + 1, :] = attended[h : h + 1]
@@ -358,18 +361,6 @@
         lhs_v[2 * n : 2 * n + 2, 0:128] = recv2[n, 0]
         lhs_v[2 * n : 2 * n + 2, 128:256] = recv2[n, 1]
     lhs = lhs_v[...].astype(BF16)
-    def scatter(zl):
-        for o in range(1, 16):
-            n = rem(d16 + o, 16)
-            pltpu.make_async_remote_copy(
-                src_ref=p1send.at[zl, n],
-                dst_ref=recvp1.at[d16, zl],
-                send_sem=sp1,
-                recv_sem=rp1,
-                device_id=(s, 8 * z + div(n, 2), rem(n, 2)),
-                device_id_type=MESH,
-            ).start()
-
     for n in range(6):
         low = slice(256 * n, 256 * n + 256)
         high = slice(1536 + 256 * n, 1536 + 256 * n + 256)
@@ -382,34 +373,131 @@
             dd, e = divmod(rest, 48)
             p1send[zl, dd, e : e + 16, :] = turned[16 * w : 16 * w + 16]
 
-    scatter(0)
-    scatter(1)
-    recvp1[d16] = p1send[:, d16]
-    most1 = recvp1.at[pl.ds(0, 15)]
-    wait_recv(most1, most1, sp1, rp1)
-    lane24 = lax.broadcasted_iota(jnp.int32, (24, 128), 1) < 64
-    for cs in range(2):
-        for zl in range(2):
-            part = recvp1[cs, zl].astype(F32)
-            for p in range(1, 8):
-                part = part + recvp1[2 * p + cs, zl].astype(F32)
-            a, b = part[0:24], part[24:48]
-            p2send[4 * cs + zl] = jnp.where(lane24, a, pltpu.roll(b, 64, 1)).astype(BF16)
-            p2send[4 * cs + 2 + zl] = jnp.where(lane24, pltpu.roll(a, 64, 1), b).astype(BF16)
-
-    for o in range(1, 8):
-        n = rem(z + o, 8)
+    def push_plane(chip_to, core):
+        n = 2 * chip_to + core
         pltpu.make_async_remote_copy(
-            src_ref=p2send.at[n],
-            dst_ref=recvp2.at[z],
-            send_sem=sp2,
-            recv_sem=rp2,
-            device_id=(s, 8 * n + chip, c),
+            src_ref=p1send.at[:, n],
+            dst_ref=recvp1.at[d16],
+            send_sem=sp1,
+            recv_sem=rp1,
+            device_id=(s, 8 * z + chip_to, core),
             device_id_type=MESH,
         ).start()
-    recvp2[z] = p2send[z]
+
+    def chip_at(dx, dy):
+        return 4 * rem(y + dy, 2) + rem(x + dx, 4)
+
+    steps = ((2, 1), (2, 0), (1, 1), (3, 1), (1, 0), (3, 0), (0, 1))
+    for parity in range(2):
+
+        @pl.when(odd == parity)
+        def _():
+            for dx, dy in steps:
+                push_plane(chip_at(dx, dy), 0)
+                if (parity + dx + dy) % 2 == 1:
+                    push_plane(chip_at(dx, dy), 1)
+
+    @pl.when(c == 1)
+    def _():
+        push_plane(chip, 0)
+
+    @pl.when((c == 0) & (odd == 1))
+    def _():
+        push_plane(chip, 1)
+
+    lane24 = lax.broadcasted_iota(jnp.int32, (24, 128), 1) < 64
+
+    def folded(part):
+        a, b = part[0:24], part[24:48]
+        low = jnp.where(lane24, a, pltpu.roll(b, 64, 1)).astype(BF16)
+        high = jnp.where(lane24, pltpu.roll(a, 64, 1), b).astype(BF16)
+        return low, high
+
+    for n in range(4):
+        for zl in range(2):
+            low, high = folded(p1send[zl, 8 * (n % 2) + 2 * n + 1].astype(F32))
+            zsend[zl, n] = low
+            zsend[2 + zl, n] = high
+    for n in range(4):
+        there = 4 * c + n
+
+        @pl.when(there != z)
+        def _():
+            pltpu.make_async_remote_copy(
+                src_ref=zsend.at[n],
+                dst_ref=zrecv.at[z],
+                send_sem=sz,
+                recv_sem=rz,
+                device_id=(s, 8 * there + chip, c),
+                device_id_type=MESH,
+            ).start()
+
+    most1 = recvp1.at[pl.ds(0, 15)]
     most2 = recvp2.at[pl.ds(0, 7)]
-    wait_recv(most2, most2, sp2, rp2)
+    mostz = zrecv.at[pl.ds(0, 7)]
+
+    @pl.when(is_plane)
+    def _():
+        recvp1[d16] = p1send[:, d16]
+        wait_recv(most1, most1, sp1, rp1)
+        for cs in range(2):
+            for zl in range(2):
+                part = recvp1[cs, zl].astype(F32)
+                for p in range(1, 8):
+                    part = part + recvp1[2 * p + cs, zl].astype(F32)
+                low, high = folded(part)
+                p2send[4 * cs + zl] = low
+                p2send[4 * cs + 2 + zl] = high
+        for o in (4, 3, 5, 2, 6, 1, 7):
+            n = rem(z + o, 8)
+            pltpu.make_async_remote_copy(
+                src_ref=p2send.at[n],
+                dst_ref=recvp2.at[z],
+                send_sem=sp2,
+                recv_sem=rp2,
+                device_id=(s, 8 * n + chip, c),
+                device_id_type=MESH,
+            ).start()
+        recvp2[z] = p2send[z]
+
+    @pl.when(is_line)
+    def _():
+        zrecv[z] = zsend[rem(z, 4)]
+        wait_recv(mostz, mostz, sz, rz)
+        for n in range(4):
+            part = zrecv[0, n].astype(F32)
+            for p in range(1, 8):
+                part = part + zrecv[p, n].astype(F32)
+            zsum[n] = part.astype(BF16)
+        for n in range(4):
+            to = 4 * (n % 2) + n
+            mine_too = (c == 1) & (chip == to)
+
+            @pl.when(jnp.logical_not(mine_too))
+            def _():
+                pltpu.make_async_remote_copy(
+                    src_ref=zsum.at[n],
+                    dst_ref=recvp2.at[chip],
+                    send_sem=sz2,
+                    recv_sem=rp2,
+                    device_id=(s, 8 * z + to, 1),
+                    device_id_type=MESH,
+                ).start()
+
+            @pl.when(mine_too)
+            def _():
+                recvp2[chip] = zsum[n]
+
+    eight = jnp.logical_not(is_plane) & (z < 4)
+
+    @pl.when(eight)
+    def _():
+        wait_recv(recvp2, recvp2, sp2, rp2)
+
+    @pl.when(jnp.logical_not(eight))
+    def _():
+        wait_recv(most2, most2, sp2, rp2)
+
     last = recvp2[0].astype(F32)
     for n in range(1, 8):
         last = last + recvp2[n].astype(F32)
@@ -429,8 +517,30 @@
             wait_send(part, part, s1, r1)
 
     wait_send(most, most, s2, r2)
-    wait_send(most1, most1, sp1, rp1)
-    wait_send(most2, most2, sp2, rp2)
+    for count, when in ((11, is_plane), (12, jnp.logical_not(is_plane))):
+
+        @pl.when(when)
+        def _():
+            part = recvp1.at[pl.ds(0, count)]
+            wait_send(part, part, sp1, rp1)
+
+    for count, when in ((3, is_line), (4, jnp.logical_not(is_line))):
+
+        @pl.when(when)
+        def _():
+            part = zrecv.at[pl.ds(0, count)]
+            wait_send(part, part, sz, rz)
+
+    @pl.when(is_plane)
+    def _():
+        wait_send(most2, most2, sp2, rp2)
+
+    for count, when in ((4, is_plane), (3, jnp.logical_not(is_plane))):
+
+        @pl.when(is_line & when)
+        def _():
+            part = recvp2.at[pl.ds(0, count)]
+            wait_send(part, part, sz2, rp2)
 
 
 def body(
@@ -477,10 +587,14 @@
             pltpu.SMEM((64,), jnp.int32),
             pltpu.SMEM((64,), jnp.int32),
             V((1, 128), F32),
+            V((2, 8, WIN), F32),
+            V((4, 4, 24, 128), BF16),
+            V((8, 4, 24, 128), BF16),
+            V((4, 24, 128), BF16),
             dma((15,)),
             dma, dma,
             dma((2,)), dma((2,)),
-            dma, dma, dma, dma, dma, dma, dma, dma, dma, dma,
+            dma, dma, dma, dma, dma, dma, dma, dma, dma, dma, dma, dma, dma,
         ],
         compiler_params=pltpu.CompilerParams(
             collective_id=0, has_side_effects=True, vmem_limit_bytes=60 * 1024 * 1024

time: 39.1 us -> 37.8 us (0.967)
  Pallas kernels: 38.4 us -> 37.1 us
    pallas_call x1, Pallas kernels: 38.4 us -> 37.1 us  [body(): pl.pallas_call(kernel, out_shape=pltpu.VMEM((48, 64), BF16), in_specs=[hb...]
where the time goes in v4:
time: 37.8 us; the launch traced here: 37.7 us
  Pallas kernels  37.1 us (98%)
  local copies, waits for them, and re-layouts  0.6 us (2%)
    pallas_call x1, Pallas kernels, body(): pl.pallas_call(kernel, out_shape=pltpu.VMEM((48, 64), BF16), in_specs=[hb...  37.1 us

profile of v4, /device:TPU:1, one launch (start us, length us, event | category | flops | bytes accessed | tf_op | source)
XLA Modules:
  0.0 37.7 jit_solution(1778473165372463394)
XLA Ops:
  0.0 37.1 %layer.1 = bf16[48,64]{1,0:T(8,128)(2,1)S(1)} custom-call(bf16[64,12288]{1,0:T(8,128)(2,1)} %hidden.1, f32[96,128]{1,0:T(8,128)} %bitcast.9, bf16[112,6144]{1,0:T(8,128)(2,1)} %bitcast.8, bf16[96,6144]{1,0:T(8,128)(2,1)} %out_w.1, bf16[136,6144]{1,0:T(8,128)(2,1)} %bitcast.6, bf16[136,6144]{1,0:T(8,128)(2,1)} %bitcast.7, bf16[136,6144]{1,0:T(8,128)(2,1)} %down.1, ...), custom_call_target="tpu_custom_call" | custom-call | tf_op jit(solution)/shard_map/layer/pallas_call | solution.py:555
  37.1 0.6 %copy.14 = bf16[64,48]{0,1:T(8,128)(2,1)} copy(bf16[64,48]{0,1:T(8,128)(2,1)S(1)} %bitcast.5) | data formatting | bytes 12288

commit v5 on v3

--- a/solution.py
+++ b/solution.py
@@ -20,7 +20,7 @@
 FFB = 136
 OB = 96
 NCOL = 3072
-SCALE = 1.0 / math.sqrt(HD)
+SCALE2 = 1.0 / math.sqrt(HD) / math.log(2.0)
 F32 = jnp.float32
 BF16 = jnp.bfloat16
 
@@ -41,8 +41,8 @@
     hidden, gain, qkv, out_w, gate, up, down, keys, values, pos_h, slots_h, freq_h, out,
     hid_v, gain_v, qkv_v, wo_v, gate_v, up_v, wd_v, k_v, v_v, normed_v,
     send1, recv1, qrow, cs_v, att_v, recv2, lhs_v, gu_send, gu_recv, act_v, acc_v,
-    p1send, recvp1, p2send, recvp2, res_v, pos, slots, freq,
-    load_sem, s1, r1, spre, rpre, s2, r2, s3, r3, s4, r4, sp1, rp1, sp2, rp2,
+    p1send, recvp1, p2send, recvp2, res_v, pos, slots, freq, bias_v, line1, zsend, zrecv, zsum, recvz2, score_v,
+    load_sem, s1, r1, spre, rpre, s2, r2, s3, r3, s4, r4, sp1, rp1, sp2, rp2, sz, rz, sz2, rz2,
 ):
     s = lax.axis_index("side")
     g = lax.axis_index("grp")
@@ -52,6 +52,8 @@
     j = 2 * g + c
     d16 = 2 * chip + c
     row_off = 64 * (rem(chip, 2))
+    x, y = rem(chip, 4), div(chip, 4)
+    is_line = c == div(z, 4)
 
     def load(src, dst, n):
         cp = pltpu.make_async_copy(src, dst, load_sem.at[n])
@@ -249,6 +251,10 @@
         cs_v[2 * r : 2 * r + 1, :] = jnp.cos(angle)
         cs_v[2 * r + 1 : 2 * r + 2, :] = jnp.where(lane1 < 64, -sine, sine)
     qrow[...] = jnp.zeros((2, 16, 128), F32)
+    column = lax.broadcasted_iota(jnp.int32, (8, WIN), 1)
+    for r in range(2):
+        age = (slots[row0 + r] - column) & (WIN - 1)
+        bias_v[r] = jnp.where((age > 0) & (age <= pos[row0 + r]), 0.0, MASKED)
 
     def wait_recv(src, dst, send, recv):
         pltpu.make_async_remote_copy(
@@ -279,29 +285,35 @@
 
     k_cp.wait()
     v_cp.wait()
-    column = lax.broadcasted_iota(jnp.int32, (16, WIN), 1)
+    rows = []
     for r in range(2):
-        x = qrow[r]
-        turned = x * cs_v[2 * r : 2 * r + 1, :] + pltpu.roll(x, 64, 1) * cs_v[2 * r + 1 : 2 * r + 2, :]
+        heads = qrow[r]
+        turned = heads * cs_v[2 * r : 2 * r + 1, :] + pltpu.roll(heads, 64, 1) * cs_v[2 * r + 1 : 2 * r + 2, :]
         query = turned.astype(BF16)
         rounded = query.astype(F32)
-        new_key = rounded[12:13]
-        new_value = x[13:14]
-        slot_r = slots[row0 + r]
-        pos_r = pos[row0 + r]
-        hit = column == slot_r
-        fresh = jnp.sum(rounded * new_key, axis=1, keepdims=True) * SCALE
-        scores = lax.dot_general(query, k_v[r], NT, preferred_element_type=F32) * SCALE
-        scores = jnp.where(hit, fresh, scores)
-        usable = ((slot_r - column) & (WIN - 1)) <= pos_r
-        scores = jnp.where(usable, scores, MASKED)
-        highest = jnp.max(scores, axis=1, keepdims=True)
-        weights = jnp.exp(scores - highest)
-        denom = jnp.sum(weights, axis=1, keepdims=True)
-        stale = jnp.where(hit, 0.0, weights).astype(BF16)
-        summed = jnp.dot(stale, v_v[r], preferred_element_type=F32)
-        own = jnp.exp(fresh - highest).astype(BF16).astype(F32)
-        attended = ((summed + own * new_value) / denom).astype(BF16).astype(F32)
+        fresh = jnp.sum(rounded * rounded[12:13], axis=1, keepdims=True)
+        highest = fresh
+        for n in range(4):
+            part = slice(1024 * n, 1024 * n + 1024)
+            bias = bias_v[r, :, part]
+            scores = lax.dot_general(query, k_v[r, part, :], NT, preferred_element_type=F32)
+            scores = scores + jnp.concatenate([bias, bias], axis=0)
+            score_v[r, :, part] = scores
+            highest = jnp.maximum(highest, jnp.max(scores, axis=1, keepdims=True))
+        rows.append((heads[13:14], fresh, highest))
+    for r in range(2):
+        new_value, fresh, highest = rows[r]
+        own = jnp.exp2((fresh - highest) * SCALE2)
+        denom = own
+        summed = own.astype(BF16).astype(F32) * new_value
+        for n in range(4):
+            part = slice(1024 * n, 1024 * n + 1024)
+            weights = jnp.exp2((score_v[r, :, part] - highest) * SCALE2)
+            denom = denom + jnp.sum(weights, axis=1, keepdims=True)
+            summed = summed + jnp.dot(
+                weights.astype(BF16), v_v[r, part, :], preferred_element_type=F32
+            )
+        attended = (summed / denom).astype(BF16).astype(F32)
         for h in range(12):
             att_v[h, r : r + 1, :] = attended[h : h + 1]
 
@@ -358,18 +370,6 @@
         lhs_v[2 * n : 2 * n + 2, 0:128] = recv2[n, 0]
         lhs_v[2 * n : 2 * n + 2, 128:256] = recv2[n, 1]
     lhs = lhs_v[...].astype(BF16)
-    def scatter(zl):
-        for o in range(1, 16):
-            n = rem(d16 + o, 16)
-            pltpu.make_async_remote_copy(
-                src_ref=p1send.at[zl, n],
-                dst_ref=recvp1.at[d16, zl],
-                send_sem=sp1,
-                recv_sem=rp1,
-                device_id=(s, 8 * z + div(n, 2), rem(n, 2)),
-                device_id_type=MESH,
-            ).start()
-
     for n in range(6):
         low = slice(256 * n, 256 * n + 256)
         high = slice(1536 + 256 * n, 1536 + 256 * n + 256)
@@ -380,24 +380,69 @@
             at = 256 * n + 16 * w
             zl, rest = divmod(at, 768)
             dd, e = divmod(rest, 48)
-            p1send[zl, dd, e : e + 16, :] = turned[16 * w : 16 * w + 16]
-
-    scatter(0)
-    scatter(1)
+            if e == 0:
+                line1[zl, dd] = turned[16 * w : 16 * w + 16]
+            else:
+                p1send[zl, dd, e - 16 : e, :] = turned[16 * w : 16 * w + 16]
+
+    def push_plane(chip_to, core):
+        n = 2 * chip_to + core
+        pltpu.make_async_remote_copy(
+            src_ref=p1send.at[:, n],
+            dst_ref=recvp1.at[d16],
+            send_sem=sp1,
+            recv_sem=rp1,
+            device_id=(s, 8 * z + chip_to, core),
+            device_id_type=MESH,
+        ).start()
+
+    for dx, dy in ((2, 1), (2, 0), (1, 1), (3, 1), (1, 0), (3, 0), (0, 1)):
+        chip_to = 4 * rem(y + dy, 2) + rem(x + dx, 4)
+        push_plane(chip_to, 0)
+        push_plane(chip_to, 1)
+    push_plane(chip, 1 - c)
+
+    def folded(part):
+        half = part.shape[0] // 2
+        left = lax.broadcasted_iota(jnp.int32, (half, 128), 1) < 64
+        a, b = part[:half], part[half:]
+        low = jnp.where(left, a, pltpu.roll(b, 64, 1)).astype(BF16)
+        high = jnp.where(left, pltpu.roll(a, 64, 1), b).astype(BF16)
+        return low, high
+
+    for n in range(16):
+        for zl in range(2):
+            low, high = folded(line1[zl, n].astype(F32))
+            zsend[zl, n] = low
+            zsend[2 + zl, n] = high
+    for n in range(4):
+        there = 4 * c + n
+
+        @pl.when(there != z)
+        def _():
+            pltpu.make_async_remote_copy(
+                src_ref=zsend.at[n],
+                dst_ref=zrecv.at[z],
+                send_sem=sz,
+                recv_sem=rz,
+                device_id=(s, 8 * there + chip, c),
+                device_id_type=MESH,
+            ).start()
+
+    most1 = recvp1.at[pl.ds(0, 15)]
+    most2 = recvp2.at[pl.ds(0, 7)]
+    mostz = zrecv.at[pl.ds(0, 7)]
     recvp1[d16] = p1send[:, d16]
-    most1 = recvp1.at[pl.ds(0, 15)]
     wait_recv(most1, most1, sp1, rp1)
-    lane24 = lax.broadcasted_iota(jnp.int32, (24, 128), 1) < 64
     for cs in range(2):
         for zl in range(2):
             part = recvp1[cs, zl].astype(F32)
             for p in range(1, 8):
                 part = part + recvp1[2 * p + cs, zl].astype(F32)
-            a, b = part[0:24], part[24:48]
-            p2send[4 * cs + zl] = jnp.where(lane24, a, pltpu.roll(b, 64, 1)).astype(BF16)
-            p2send[4 * cs + 2 + zl] = jnp.where(lane24, pltpu.roll(a, 64, 1), b).astype(BF16)
-
-    for o in range(1, 8):
+            low, high = folded(part)
+            p2send[4 * cs + zl] = low
+            p2send[4 * cs + 2 + zl] = high
+    for o in (4, 3, 5, 2, 6, 1, 7):
         n = rem(z + o, 8)
         pltpu.make_async_remote_copy(
             src_ref=p2send.at[n],
@@ -408,12 +453,44 @@
             device_id_type=MESH,
         ).start()
     recvp2[z] = p2send[z]
-    most2 = recvp2.at[pl.ds(0, 7)]
+
+    @pl.when(is_line)
+    def _():
+        zrecv[z] = zsend[rem(z, 4)]
+        wait_recv(mostz, mostz, sz, rz)
+        for n in range(16):
+            part = zrecv[0, n].astype(F32)
+            for p in range(1, 8):
+                part = part + zrecv[p, n].astype(F32)
+            zsum[n] = part.astype(BF16)
+        for o in range(1, 16):
+            n = rem(d16 + o, 16)
+            pltpu.make_async_remote_copy(
+                src_ref=zsum.at[n],
+                dst_ref=recvz2.at[chip],
+                send_sem=sz2,
+                recv_sem=rz2,
+                device_id=(s, 8 * z + div(n, 2), rem(n, 2)),
+                device_id_type=MESH,
+            ).start()
+        recvz2[chip] = zsum[d16]
+        seven = recvz2.at[pl.ds(0, 7)]
+        wait_recv(seven, seven, sz2, rz2)
+
+    @pl.when(jnp.logical_not(is_line))
+    def _():
+        wait_recv(recvz2, recvz2, sz2, rz2)
+
     wait_recv(most2, most2, sp2, rp2)
     last = recvp2[0].astype(F32)
     for n in range(1, 8):
         last = last + recvp2[n].astype(F32)
-    result = jnp.concatenate([last, pltpu.roll(last, 64, 1)], axis=0)[:, 0:64]
+    line = recvz2[0].astype(F32)
+    for n in range(1, 8):
+        line = line + recvz2[n].astype(F32)
+    result = jnp.concatenate(
+        [line, pltpu.roll(line, 64, 1), last, pltpu.roll(last, 64, 1)], axis=0
+    )[:, 0:64]
     out[...] = (result + res_v[pl.ds(res_off, 48), :]).astype(BF16)
 
     for count, when in (
@@ -431,6 +508,17 @@
     wait_send(most, most, s2, r2)
     wait_send(most1, most1, sp1, rp1)
     wait_send(most2, most2, sp2, rp2)
+    for count, when in ((3, is_line), (4, jnp.logical_not(is_line))):
+
+        @pl.when(when)
+        def _():
+            part = zrecv.at[pl.ds(0, count)]
+            wait_send(part, part, sz, rz)
+
+    @pl.when(is_line)
+    def _():
+        part = zsum.at[pl.ds(0, 15)]
+        wait_send(part, part, sz2, rz2)
 
 
 def body(
@@ -469,18 +557,25 @@
             V((FFB, 128), F32),
             V((2, FFB, 128), BF16),
             V((64, NCOL), F32),
-            V((2, 16, 48, 128), BF16),
-            V((16, 2, 48, 128), BF16),
-            V((8, 24, 128), BF16),
-            V((8, 24, 128), BF16),
+            V((2, 16, 32, 128), BF16),
+            V((16, 2, 32, 128), BF16),
+            V((8, 16, 128), BF16),
+            V((8, 16, 128), BF16),
             V((256, 64), F32),
             pltpu.SMEM((64,), jnp.int32),
             pltpu.SMEM((64,), jnp.int32),
             V((1, 128), F32),
+            V((2, 8, WIN), F32),
+            V((2, 16, 16, 128), BF16),
+            V((4, 16, 8, 128), BF16),
+            V((8, 16, 8, 128), BF16),
+            V((16, 8, 128), BF16),
+            V((8, 8, 128), BF16),
+            V((2, 16, WIN), F32),
             dma((15,)),
             dma, dma,
             dma((2,)), dma((2,)),
-            dma, dma, dma, dma, dma, dma, dma, dma, dma, dma,
+            dma, dma, dma, dma, dma, dma, dma, dma, dma, dma, dma, dma, dma, dma,
         ],
         compiler_params=pltpu.CompilerParams(
             collective_id=0, has_side_effects=True, vmem_limit_bytes=60 * 1024 * 1024

time: 39.1 us -> 37.5 us (0.959)
  Pallas kernels: 38.4 us -> 36.8 us
    pallas_call x1, Pallas kernels: 38.4 us -> 36.8 us  [body(): pl.pallas_call(kernel, out_shape=pltpu.VMEM((48, 64), BF16), in_specs=[hb...]
where the time goes in v5:
time: 37.5 us; the launch traced here: 37.4 us
  Pallas kernels  36.8 us (98%)
  local copies, waits for them, and re-layouts  0.6 us (2%)
    pallas_call x1, Pallas kernels, body(): pl.pallas_call(kernel, out_shape=pltpu.VMEM((48, 64), BF16), in_specs=[hb...  36.8 us

profile of v5, /device:TPU:1, one launch (start us, length us, event | category | flops | bytes accessed | tf_op | source)
XLA Modules:
  0.0 37.4 jit_solution(12730470237003758931)
XLA Ops:
  0.0 36.8 %layer.1 = bf16[48,64]{1,0:T(8,128)(2,1)S(1)} custom-call(bf16[64,12288]{1,0:T(8,128)(2,1)} %hidden.1, f32[96,128]{1,0:T(8,128)} %bitcast.9, bf16[112,6144]{1,0:T(8,128)(2,1)} %bitcast.8, bf16[96,6144]{1,0:T(8,128)(2,1)} %out_w.1, bf16[136,6144]{1,0:T(8,128)(2,1)} %bitcast.6, bf16[136,6144]{1,0:T(8,128)(2,1)} %bitcast.7, bf16[136,6144]{1,0:T(8,128)(2,1)} %down.1, ...), custom_call_target="tpu_custom_call" | custom-call | tf_op jit(solution)/shard_map/layer/pallas_call | solution.py:533
  36.8 0.6 %copy.14 = bf16[64,48]{0,1:T(8,128)(2,1)} copy(bf16[64,48]{0,1:T(8,128)(2,1)S(1)} %bitcast.5) | data formatting | bytes 12288

commit v6 on v5

--- a/solution.py
+++ b/solution.py
@@ -20,6 +20,7 @@
 FFB = 136
 OB = 96
 NCOL = 3072
+PARTS = 8
 SCALE2 = 1.0 / math.sqrt(HD) / math.log(2.0)
 F32 = jnp.float32
 BF16 = jnp.bfloat16
@@ -41,7 +42,7 @@
     hidden, gain, qkv, out_w, gate, up, down, keys, values, pos_h, slots_h, freq_h, out,
     hid_v, gain_v, qkv_v, wo_v, gate_v, up_v, wd_v, k_v, v_v, normed_v,
     send1, recv1, qrow, cs_v, att_v, recv2, lhs_v, gu_send, gu_recv, act_v, acc_v,
-    p1send, recvp1, p2send, recvp2, res_v, pos, slots, freq, bias_v, line1, zsend, zrecv, zsum, recvz2, score_v,
+    p1send, recvp1, p2send, recvp2, res_v, pos, slots, freq, bias_v, line1, zsend, zrecv, zsum, recvz2, score_v, kt_v,
     load_sem, s1, r1, spre, rpre, s2, r2, s3, r3, s4, r4, sp1, rp1, sp2, rp2, sz, rz, sz2, rz2,
 ):
     s = lax.axis_index("side")
@@ -104,7 +105,9 @@
     gate_cp = load(gate, gate_v, 6)
     up_cp = load(up, up_v, 7)
     k_cp = load(keys, k_v, 8)
-    v_cp = load(values, v_v, 9)
+    kv_cp = [
+        load(values.at[r], v_v.at[:, pl.ds(HD * r, HD)], 15 + r) for r in range(2)
+    ]
     own_cols = pl.ds(pl.multiple_of(NCOL * c, NCOL), NCOL)
     wo_cp = load(
         out_w.at[:, own_cols], wo_v.at[pl.ds(pl.multiple_of(row_off + OB * c, 32), OB)], 10
@@ -251,6 +254,11 @@
         cs_v[2 * r : 2 * r + 1, :] = jnp.cos(angle)
         cs_v[2 * r + 1 : 2 * r + 2, :] = jnp.where(lane1 < 64, -sine, sine)
     qrow[...] = jnp.zeros((2, 16, 128), F32)
+    k_cp.wait()
+    for r in range(2):
+        for n in range(8):
+            part = slice(512 * n, 512 * n + 512)
+            kt_v[HD * r : HD * r + HD, part] = k_v[r, part, :].T
     column = lax.broadcasted_iota(jnp.int32, (8, WIN), 1)
     for r in range(2):
         age = (slots[row0 + r] - column) & (WIN - 1)
@@ -283,39 +291,48 @@
         qrow[0, cc : cc + 1, :] = both[0:1]
         qrow[1, cc : cc + 1, :] = both[1:2]
 
-    k_cp.wait()
-    v_cp.wait()
-    rows = []
+    for cp in kv_cp:
+        cp.wait()
+    queries, news, fresh = [], [], []
+    blank = jnp.zeros((16, 128), BF16)
     for r in range(2):
         heads = qrow[r]
         turned = heads * cs_v[2 * r : 2 * r + 1, :] + pltpu.roll(heads, 64, 1) * cs_v[2 * r + 1 : 2 * r + 2, :]
         query = turned.astype(BF16)
         rounded = query.astype(F32)
-        fresh = jnp.sum(rounded * rounded[12:13], axis=1, keepdims=True)
-        highest = fresh
-        for n in range(4):
-            part = slice(1024 * n, 1024 * n + 1024)
-            bias = bias_v[r, :, part]
-            scores = lax.dot_general(query, k_v[r, part, :], NT, preferred_element_type=F32)
-            scores = scores + jnp.concatenate([bias, bias], axis=0)
-            score_v[r, :, part] = scores
-            highest = jnp.maximum(highest, jnp.max(scores, axis=1, keepdims=True))
-        rows.append((heads[13:14], fresh, highest))
-    for r in range(2):
-        new_value, fresh, highest = rows[r]
-        own = jnp.exp2((fresh - highest) * SCALE2)
-        denom = own
-        summed = own.astype(BF16).astype(F32) * new_value
-        for n in range(4):
-            part = slice(1024 * n, 1024 * n + 1024)
-            weights = jnp.exp2((score_v[r, :, part] - highest) * SCALE2)
-            denom = denom + jnp.sum(weights, axis=1, keepdims=True)
-            summed = summed + jnp.dot(
-                weights.astype(BF16), v_v[r, part, :], preferred_element_type=F32
-            )
-        attended = (summed / denom).astype(BF16).astype(F32)
-        for h in range(12):
-            att_v[h, r : r + 1, :] = attended[h : h + 1]
+        fresh.append(jnp.sum(rounded * rounded[12:13], axis=1, keepdims=True))
+        queries.append(jnp.concatenate([query, blank] if r == 0 else [blank, query], axis=1))
+        news.append(heads[13:14])
+    query = jnp.concatenate(queries, axis=0)
+    fresh = jnp.concatenate(fresh, axis=0)
+    highest = fresh
+    for n in range(PARTS):
+        part = slice(WIN // PARTS * n, WIN // PARTS * (n + 1))
+        scores = jnp.dot(query, kt_v[:, part], preferred_element_type=F32)
+        bias = [bias_v[r, :, part] for r in (0, 0, 1, 1)]
+        scores = scores + jnp.concatenate(bias, axis=0)
+        score_v[:, part] = scores
+        highest = jnp.maximum(highest, jnp.max(scores, axis=1, keepdims=True))
+    own = jnp.exp2((fresh - highest) * SCALE2)
+    denom = own
+    summed = jnp.zeros((32, 256), F32)
+    for n in range(PARTS):
+        part = slice(WIN // PARTS * n, WIN // PARTS * (n + 1))
+        weights = jnp.exp2((score_v[:, part] - highest) * SCALE2)
+        denom = denom + jnp.sum(weights, axis=1, keepdims=True)
+        summed = summed + jnp.dot(
+            weights.astype(BF16), v_v[part, :], preferred_element_type=F32
+        )
+    own = own.astype(BF16).astype(F32)
+    attended = [
+        (summed[16 * r : 16 * r + 16, HD * r : HD * r + HD] + own[16 * r : 16 * r + 16] * news[r])
+        / denom[16 * r : 16 * r + 16]
+        for r in range(2)
+    ]
+    for h in range(12):
+        att_v[h] = jnp.concatenate(
+            [attended[0][h : h + 1], attended[1][h : h + 1]], axis=0
+        ).astype(BF16)
 
     here = s * 16 + d16
 
@@ -330,11 +347,14 @@
             device_id_type=MESH,
         ).start()
 
-    for o in range(16):
-        i = rem(d16 + o, 16)
-        spread_heads(1 - s, i)
-        if o > 0:
-            spread_heads(s, i)
+    for dx in (2, 1, 3, 0):
+        for side, dy in ((1 - s, 0), (1 - s, 1), (s, 1), (s, 0)):
+            i = 2 * (4 * rem(y + dy, 2) + rem(x + dx, 4))
+            if dx == 0 and dy == 0 and side is s:
+                spread_heads(s, i + 1 - c)
+            else:
+                spread_heads(side, i)
+                spread_heads(side, i + 1)
     recv2[here] = att_v[pl.ds(div(3 * chip, 2), 2)]
 
     gu.wait()
@@ -367,8 +387,8 @@
     most = recv2.at[pl.ds(0, 31)]
     wait_recv(most, most, s2, r2)
     for n in range(32):
-        lhs_v[2 * n : 2 * n + 2, 0:128] = recv2[n, 0]
-        lhs_v[2 * n : 2 * n + 2, 128:256] = recv2[n, 1]
+        lhs_v[2 * n : 2 * n + 2, 0:128] = recv2[n, 0].astype(F32)
+        lhs_v[2 * n : 2 * n + 2, 128:256] = recv2[n, 1].astype(F32)
     lhs = lhs_v[...].astype(BF16)
     for n in range(6):
         low = slice(256 * n, 256 * n + 256)
@@ -544,14 +564,14 @@
             V((FFB, HALF), BF16),
             V((2, FFB, NCOL), BF16),
             V((2, WIN, HD), BF16),
-            V((2, WIN, HD), BF16),
+            V((WIN, 2 * HD), BF16),
             V((64, HALF), BF16),
             V((64, 2, 128), F32),
             V((56, 2, 128), F32),
             V((2, 16, 128), F32),
             V((8, 128), F32),
-            V((12, 2, 128), F32),
-            V((32, 2, 2, 128), F32),
+            V((12, 2, 128), BF16),
+            V((32, 2, 2, 128), BF16),
             V((64, 256), F32),
             V((FFB, 128), F32),
             V((FFB, 128), F32),
@@ -571,8 +591,9 @@
             V((8, 16, 8, 128), BF16),
             V((16, 8, 128), BF16),
             V((8, 8, 128), BF16),
-            V((2, 16, WIN), F32),
-            dma((15,)),
+            V((32, WIN), F32),
+            V((2 * HD, WIN), BF16),
+            dma((17,)),
             dma, dma,
             dma((2,)), dma((2,)),
             dma, dma, dma, dma, dma, dma, dma, dma, dma, dma, dma, dma, dma, dma,

time: 37.5 us -> 37.3 us (level)
  no operation moved by 1% of the time
where the time goes in v6:
time: 37.3 us; the launch traced here: 37.2 us
  Pallas kernels  36.6 us (98%)
  local copies, waits for them, and re-layouts  0.6 us (2%)
    pallas_call x1, Pallas kernels, body(): pl.pallas_call(kernel, out_shape=pltpu.VMEM((48, 64), BF16), in_specs=[hb...  36.6 us

profile of v6, /device:TPU:1, one launch (start us, length us, event | category | flops | bytes accessed | tf_op | source)
XLA Modules:
  0.0 37.2 jit_solution(1140657262694718020)
XLA Ops:
  0.0 36.6 %layer.1 = bf16[48,64]{1,0:T(8,128)(2,1)S(1)} custom-call(bf16[64,12288]{1,0:T(8,128)(2,1)} %hidden.1, f32[96,128]{1,0:T(8,128)} %bitcast.9, bf16[112,6144]{1,0:T(8,128)(2,1)} %bitcast.8, bf16[96,6144]{1,0:T(8,128)(2,1)} %out_w.1, bf16[136,6144]{1,0:T(8,128)(2,1)} %bitcast.6, bf16[136,6144]{1,0:T(8,128)(2,1)} %bitcast.7, bf16[136,6144]{1,0:T(8,128)(2,1)} %down.1, ...), custom_call_target="tpu_custom_call" | custom-call | tf_op jit(solution)/shard_map/layer/pallas_call | solution.py:553
  36.6 0.6 %copy.14 = bf16[64,48]{0,1:T(8,128)(2,1)} copy(bf16[64,48]{0,1:T(8,128)(2,1)S(1)} %bitcast.5) | data formatting | bytes 12288
